TPU v7x, 16 devices: a whole 2x2x2 slice. The times are simulated.
16 devices in a mesh: dp: 4 (over z, y), tp: 4 (over x, core).
Axes of the slice: x: 2, y: 2, z: 2, core: 2. Of those that a mesh axis runs over, the one named last changes fastest.
Arguments:
- x: bfloat16 [2048, 2048], P('dp'), parts along dimension 0
- k_cache: bfloat16 [2048, 16, 16, 128], P('dp', None, 'tp'), parts along dimension 0
- v_cache: bfloat16 [2048, 16, 16, 128], P('dp', None, 'tp'), parts along dimension 0
- positions: int32 [2048], P('dp'), parts along dimension 0
- att_ids: int32 [2048, 2], P('dp'), parts along dimension 0
- mlp_ids: int32 [2048, 2], P('dp'), parts along dimension 0
- norm_att: float32 [2048], replicated
- w_kv: bfloat16 [2048, 16, 256], P(None, 'tp')
- router_att: bfloat16 [2048, 8], replicated
- w_query: bfloat16 [8, 2048, 2048], P(None, None, 'tp')
- w_out: bfloat16 [8, 2048, 2048], P(None, 'tp')
- norm_mlp: float32 [2048], replicated
- router_mlp: bfloat16 [2048, 8], replicated
- w_gate: bfloat16 [8, 2048, 5632], P('tp')
- w_up: bfloat16 [8, 2048, 5632], P('tp')
- w_down: bfloat16 [8, 5632, 2048], P('tp')
Outputs:
- output 1: bfloat16 [2048, 2048], P('dp'), parts along dimension 0
- output 2: bfloat16 [2048, 16, 16, 128], P('dp', None, 'tp'), parts along dimension 0
- output 3: bfloat16 [2048, 16, 16, 128], P('dp', None, 'tp'), parts along dimension 0
There are 4 independent parts. A program takes and returns all parts, laid end to end along the dimension named above; an argument that names none is the same for every part.
All inputs are finite; a program needn't handle non-finite values.
Results may differ from a plain program's by a relative error of at most 0.0123415.
Values are sent between devices in bfloat16 or wider.
A program may use at most 1 GiB of HBM per device.

v0:
```python
import jax
import jax.numpy as jnp
from jax import lax
from jax.sharding import PartitionSpec as P

NORM_EPS = 1e-6
ROPE_BASE = 10000.0


def rms_norm(x, gain):
    values = x.astype(jnp.float32)
    inv_rms = lax.rsqrt(jnp.mean(values * values, axis=-1, keepdims=True) + NORM_EPS)
    return (values * inv_rms * gain).astype(jnp.bfloat16)


def rope_tables(positions, head_dim):
    half_dim = head_dim // 2
    inv_freq = ROPE_BASE ** (-(jnp.arange(half_dim, dtype=jnp.float32) * 2.0 / head_dim))
    angles = positions.astype(jnp.float32)[:, None] * inv_freq[None, :]
    return jnp.cos(angles), jnp.sin(angles)


def apply_rope(vectors, cos_table, sin_table):
    half_dim = vectors.shape[-1] // 2
    first_half = vectors[..., :half_dim]
    second_half = vectors[..., half_dim:]
    return jnp.concatenate([first_half * cos_table - second_half * sin_table, second_half * cos_table + first_half * sin_table], axis=-1)


def route_weights(logits, choice_ids, first_id, count):
    pair_gates = jax.nn.softmax(jnp.take_along_axis(logits, choice_ids, axis=1), axis=-1)
    expert_index = first_id + jnp.arange(count)
    onehot = (choice_ids[:, :, None] == expert_index[None, None, :]).astype(jnp.float32)
    dense_gates = jnp.sum(onehot * pair_gates[:, :, None], axis=1)
    return onehot, dense_gates


def attention_part(hidden, k_cache, v_cache, positions, att_ids, w_kv, router_att, w_query, w_out):
    tokens = hidden.shape[0]
    head_count = k_cache.shape[2]
    head_dim = k_cache.shape[3]
    kv_new = jnp.einsum('bd,dnc->bnc', hidden, w_kv, preferred_element_type=jnp.float32)
    cos_table, sin_table = rope_tables(positions, head_dim)
    key_new = apply_rope(kv_new[:, :, :head_dim], cos_table[:, None, :], sin_table[:, None, :]).astype(jnp.bfloat16)
    value_new = kv_new[:, :, head_dim:].astype(jnp.bfloat16)
    slot_index = jnp.arange(k_cache.shape[1])
    at_slot = (slot_index[None, :] == positions[:, None])[:, :, None, None]
    keys_all = jnp.where(at_slot, key_new[:, None, :, :], k_cache)
    values_all = jnp.where(at_slot, value_new[:, None, :, :], v_cache)
    att_logits = jnp.dot(hidden, router_att, preferred_element_type=jnp.float32)
    att_onehot, att_dense = route_weights(att_logits, att_ids, 0, w_query.shape[0])
    query_all = jnp.einsum('bd,edc->bec', hidden, w_query, preferred_element_type=jnp.float32)
    query_sel = jnp.take_along_axis(query_all, att_ids[:, :, None], axis=1).reshape(tokens, 2, head_count, head_dim)
    query_rot = apply_rope(query_sel, cos_table[:, None, None, :], sin_table[:, None, None, :]).astype(jnp.bfloat16)
    scores = jnp.einsum('bknd,bsnd->bkns', query_rot, keys_all, preferred_element_type=jnp.float32) * head_dim ** -0.5
    visible = (slot_index[None, :] <= positions[:, None])[:, None, None, :]
    weights = jax.nn.softmax(jnp.where(visible, scores, -1e30), axis=-1).astype(jnp.bfloat16)
    attended = jnp.einsum('bkns,bsnd->bknd', weights, values_all, preferred_element_type=jnp.float32).astype(jnp.bfloat16).reshape(tokens, 2, head_count * head_dim)
    out_slots = jnp.einsum('bke,bkc->bec', att_onehot.astype(jnp.bfloat16), attended, preferred_element_type=jnp.float32).astype(jnp.bfloat16)
    projected = jnp.einsum('bec,ecd->bed', out_slots, w_out, preferred_element_type=jnp.float32)
    att_part = jnp.sum(att_dense[:, :, None] * projected, axis=1)
    return att_part, keys_all, values_all


def expert_part(normed, mlp_dense, w_gate, w_up, w_down):
    gate_val = jnp.einsum('bd,edf->bef', normed, w_gate, preferred_element_type=jnp.float32)
    up_val = jnp.einsum('bd,edf->bef', normed, w_up, preferred_element_type=jnp.float32)
    activation = (jax.nn.silu(gate_val) * up_val).astype(jnp.bfloat16)
    down_out = jnp.einsum('bef,efd->bed', activation, w_down, preferred_element_type=jnp.float32)
    return jnp.sum(mlp_dense[:, :, None] * down_out, axis=1)


def solution(mesh):
    def local_step(x, k_cache, v_cache, positions, att_ids, mlp_ids, norm_att, w_kv, router_att, w_query, w_out, norm_mlp, router_mlp, w_gate, w_up, w_down):
        hidden = rms_norm(x, norm_att)
        att_part, keys_all, values_all = attention_part(hidden, k_cache, v_cache, positions, att_ids, w_kv, router_att, w_query, w_out)
        att_sum = lax.psum(att_part.astype(jnp.bfloat16), 'tp').astype(jnp.float32)
        x_mid = (x.astype(jnp.float32) + att_sum).astype(jnp.bfloat16)
        normed = rms_norm(x_mid, norm_mlp)
        mlp_logits = jnp.dot(normed, router_mlp, preferred_element_type=jnp.float32)
        local_count = w_gate.shape[0]
        _, mlp_dense = route_weights(mlp_logits, mlp_ids, lax.axis_index('tp') * local_count, local_count)
        mlp_part = expert_part(normed, mlp_dense, w_gate, w_up, w_down)
        mlp_sum = lax.psum(mlp_part.astype(jnp.bfloat16), 'tp').astype(jnp.float32)
        x_out = (x_mid.astype(jnp.float32) + mlp_sum).astype(jnp.bfloat16)
        return x_out, keys_all, values_all

    token_spec = P('dp', None)
    cache_spec = P('dp', None, 'tp', None)
    expert_spec = P('tp', None, None)
    in_specs = (token_spec, cache_spec, cache_spec, P('dp'), token_spec, token_spec, P(), P(None, 'tp', None), P(), P(None, None, 'tp'), P(None, 'tp', None), P(), P(), expert_spec, expert_spec, expert_spec)
    out_specs = (token_spec, cache_spec, cache_spec)
    return jax.shard_map(local_step, mesh=mesh, in_specs=in_specs, out_specs=out_specs, check_vma=False)
```

profile of v0, /device:TPU:0, one launch (start us, length us, event | category | flops | bytes accessed | tf_op | source)
XLA Modules:
  0.0 366.0 jit_solution(9195990011002025046)
XLA Ops:
  7.9 1.4 iota_compare_fusion
  9.4 2.1 fusion.8
  11.5 5.3 %fusion.17 = f32[512,4,256]{0,2,1:T(8,128)S(1)} fusion(bf16[2048,4,256]{2,1,0:T(4,128)(2,1)} %param.25, bf16[512,2048]{1,0:T(8,128)(2,1)} %param.18, f32[2048]{0:T(1024)} %param.24, f32[512]{0:T(512)S(1)} %add_rsqrt_fusion.1), kind=kOutput, calls=%fused_computation.31 | convolution fusion | flops 2151677952 | bytes 8398848 | tf_op jit(solution)/shard_map/bd,dnc->bnc/dot_general | solution.py:42
  16.8 1.3 copy-done.7
  18.1 0.9 slice.44
  19.5 0.8 copy.89
  20.3 1.4 subtract_convert_fusion.1
  21.7 0.8 copy.90
  22.9 1.4 copy.83
  24.3 1.4 fusion.59
  26.1 7.0 %gather_fusion.1 = f32[1024]{0:T(1024)S(1)} fusion(f32[512,8]{0,1:T(8,128)S(1)} %fusion.59, s32[1024]{0:T(1024)S(1)} %reshape.244), kind=kCustom, calls=%fused_computation.clone | custom fusion | bytes 16384 | tf_op jit(solution)/shard_map/jit(take_along_axis)/gather | solution.py:31
  33.5 0.8 copy.85
  34.3 11.8 %fusion.29 = f32[512,8,512]{2,0,1:T(8,128)S(1)} fusion(bf16[8,2048,512]{2,1,0:T(8,128)(2,1)} %param.27, bf16[512,2048]{1,0:T(8,128)(2,1)S(1)} %copy-done.2, f32[2048]{0:T(1024)S(1)} %copy-done.16, f32[512]{0:T(512)S(1)} %add_rsqrt_fusion.1), kind=kOutput, calls=%fused_computation.42 | convolution fusion | flops 8594128896 | bytes 27273216 | tf_op jit(solution)/shard_map/bd,edc->bec/dot_general | solution.py:52
  46.1 8.3 %copy.87 = f32[512,8,512]{2,1,0:T(8,128)} copy(f32[512,8,512]{2,0,1:T(8,128)S(1)} %fusion.29) | data formatting | bytes 16777216 | tf_op jit(solution)/shard_map/bd,edc->bec/dot_general | solution.py:52
  54.4 18.3 %gather_fusion = f32[1024,512]{1,0:T(8,128)} fusion(f32[512,8,512]{2,1,0:T(8,128)} %copy.87, s32[1024]{0:T(1024)S(1)} %reshape.244), kind=kCustom, calls=%fused_computation.2 | custom fusion | bytes 4202496 | tf_op jit(solution)/shard_map/jit(take_along_axis)/gather | solution.py:53
  72.6 2.9 gather.10
  75.6 4.1 %copy_select_fusion = f32[512,2,4,128]{3,1,2,0:T(2,128)S(1)} fusion(f32[512,2,4,128]{3,2,1,0:T(4,128)} %gather.10, pred[512,2]{1,0:T(8,128)(4,1)} %copy.85), kind=kLoop, calls=%fused_computation.45 | loop fusion | flops 524288 | bytes 4195328 | tf_op jit(solution)/shard_map/jit(take_along_axis)/select_n | solution.py:53
  79.7 4.0 %subtract_convert_fusion = (bf16[512,2,4,64]{3,1,2,0:T(2,128)(2,1)}, bf16[512,2,4,64]{3,1,2,0:T(2,128)(2,1)}) fusion(f32[512,2,4,128]{3,1,2,0:T(2,128)S(1)} %copy_select_fusion, f32[512,64]{1,0:T(8,128)S(1)} %copy-done.9, f32[512,64]{1,0:T(8,128)S(1)} %copy-done.8), kind=kLoop, calls=%fused_computation.48 | loop fusion | flops 2097152 | bytes 3407872 | tf_op jit(solution)/shard_map/convert
  83.6 14.4 %broadcast_select_fusion = (bf16[512,16,4,128]{3,2,1,0:T(4,128)(2,1)}, bf16[512,16,4,128]{3,2,1,0:T(4,128)(2,1)}) fusion(bf16[512,16,4,128]{3,2,1,0:T(4,128)(2,1)} %param.19, pred[512,16]{1,0:T(8,128)(4,1)S(1)} %get-tuple-element.17, bf16[512,4,128]{2,1,0:T(4,128)(2,1)S(1)} %copy.84, bf16[512,16,4,128]{3,2,1,0:T(4,128)(2,1)} %param.20, ...), kind=kLoop, calls=%fused_computation.14 | loop fusion | flops 8388608 | bytes 34611200 | tf_op jit(solution)/shard_map/jit(_where)/select_n | solution.py:48
  98.0 9.9 %multiply_select_fusion = f32[512,4,16,2]{2,3,1,0:T(2,128)} fusion(pred[512,16]{1,0:T(8,128)(4,1)S(1)} %copy-done.11, bf16[512,16,4,128]{3,2,1,0:T(4,128)(2,1)} %get-tuple-element.12, bf16[512,2,4,64]{3,1,2,0:T(2,128)(2,1)} %get-tuple-element.9, bf16[512,2,4,64]{3,1,2,0:T(2,128)(2,1)} %get-tuple-element.8), kind=kOutput, calls=%fused_computation.46 | convolution fusion | flops 19005440 | bytes 9707520 | tf_op jit(solution)/shard_map/bknd,bsnd->bkns/dot_general | solution.py:55
  108.0 6.9 %fusion.62 = (f32[512,2,4]{1,2,0:T(4,128)S(1)}, f32[512,2,4,16]{3,1,2,0:T(2,128)}) fusion(f32[512,4,16,2]{2,3,1,0:T(2,128)} %multiply_select_fusion), kind=kOutput, calls=%fused_computation.92 | output fusion | flops 131087 | bytes 540672 | tf_op jit(solution)/shard_map/sub | solution.py:57
  115.1 8.5 %convolution_convert_fusion = bf16[512,8,512]{2,1,0:T(8,128)(2,1)} fusion(bf16[512,2,8]{2,1,0:T(2,128)(2,1)S(1)} %copy.93, bf16[512,16,4,128]{3,2,1,0:T(4,128)(2,1)} %get-tuple-element.13, f32[512,2,4,16]{3,1,2,0:T(2,128)} %get-tuple-element.19, f32[512,2,4]{1,2,0:T(4,128)S(1)} %get-tuple-element.18), kind=kOutput, calls=%fused_computation.33 | convolution fusion | flops 27918336 | bytes 12877824 | tf_op jit(solution)/shard_map/bke,bkc->bec/dot_general | solution.py:59
  123.6 20.2 %fusion.1 = bf16[512,2048]{1,0:T(8,128)(2,1)} fusion(bf16[8,512,2048]{2,1,0:T(8,128)(2,1)} %param.28, f32[512,8]{0,1:T(8,128)S(1)} %select_reduce_fusion, bf16[512,8,512]{2,1,0:T(8,128)(2,1)} %convolution_convert_fusion), kind=kOutput, calls=%fused_computation.5 | convolution fusion | flops 8605663232 | bytes 23085056 | tf_op jit(solution)/shard_map/bec,ecd->bed/dot_general | solution.py:60
  144.8 49.5 %all-reduce.3.cloned.1.call-done = bf16[512,2048]{1,0:T(8,128)(2,1)} async-done(((bf16[512,2048]{1,0:T(8,128)(2,1)}), bf16[512,2048]{1,0:T(8,128)(2,1)}) %all-reduce.3.cloned.1.call-update) | async-done | bytes 2097168 | tf_op jit(solution)/shard_map/psum | solution.py:77
  194.3 2.5 fusion.12
  196.8 1.0 fusion.14
  197.9 32.4 %fusion.21 = f32[512,2,5632]{2,0,1:T(8,128)} fusion(bf16[2,2048,5632]{2,1,0:T(8,128)(2,1)} %param.31, bf16[512,2048]{1,0:T(8,128)(2,1)S(1)} %fusion.14), kind=kOutput, calls=%fused_computation.36 | convolution fusion | flops 23622320128 | bytes 71303168 | tf_op jit(solution)/shard_map/bd,edf->bef/dot_general | solution.py:66
  230.9 6.5 %gather_fusion.2 = f32[1024]{0:T(1024)S(1)} fusion(f32[512,8]{0,1:T(8,128)S(1)} %fusion.63, s32[1024]{0:T(1024)S(1)} %reshape.249), kind=kCustom, calls=%fused_computation.1.clone | custom fusion | bytes 16384 | tf_op jit(solution)/shard_map/jit(take_along_axis)/gather | solution.py:31
  237.9 33.8 %multiply_convert_fusion.6 = bf16[512,2,5632]{2,0,1:T(8,128)(2,1)} fusion(f32[512,2,5632]{2,0,1:T(8,128)} %fusion.21, bf16[2,2048,5632]{2,1,0:T(8,128)(2,1)} %param.32, bf16[512,2048]{1,0:T(8,128)(2,1)S(1)} %copy-done.6), kind=kOutput, calls=%fused_computation.6.clone.clone.clone.clone.1 | convolution fusion | flops 23656923136 | bytes 82837504 | tf_op jit(solution)/shard_map/bd,edf->bef/dot_general | solution.py:67
  271.8 34.2 %fusion.3 = bf16[512,2048]{1,0:T(8,128)(2,1)} fusion(bf16[2,5632,2048]{2,1,0:T(8,128)(2,1)} %param.33, f32[512,2]{0,1:T(2,128)S(1)} %fusion.49, bf16[512,2,5632]{2,0,1:T(8,128)(2,1)} %multiply_convert_fusion.6), kind=kOutput, calls=%fused_computation.9 | convolution fusion | flops 23625465856 | bytes 59772928 | tf_op jit(solution)/shard_map/bef,efd->bed/dot_general | solution.py:69
  306.0 47.7 %all-reduce.5.cloned.1.call-done = bf16[512,2048]{1,0:T(8,128)(2,1)} async-done(((bf16[512,2048]{1,0:T(8,128)(2,1)}), bf16[512,2048]{1,0:T(8,128)(2,1)}) %all-reduce.5.cloned.1.call-update) | async-done | bytes 2097168 | tf_op jit(solution)/shard_map/psum | solution.py:84
  353.7 5.0 %fusion.15 = bf16[512,2048]{1,0:T(8,128)(2,1)} fusion(bf16[512,2048]{1,0:T(8,128)(2,1)} %all-reduce.5.cloned.1.call-done, bf16[512,2048]{1,0:T(8,128)(2,1)} %all-reduce.3.cloned.1.call-done, bf16[512,2048]{1,0:T(8,128)(2,1)S(1)} %copy-done.3), kind=kLoop, calls=%fused_computation.29 | loop fusion | flops 8388608 | bytes 8388608 | tf_op jit(solution)/shard_map/convert_element_type | solution.py:85
  (66 shorter events, 4.7 us)
Async XLA Ops:
  7.2 17.1 %copy-start = (bf16[2048,8]{0,1:T(8,128)(2,1)S(1)}, bf16[2048,8]{0,1:T(8,128)(2,1)}, u32[]{:S(2)}) copy-start(bf16[2048,8]{0,1:T(8,128)(2,1)} %param.26) | copy-start | bytes 98308
  7.2 187.1 %all-reduce.3.cloned.1.call-start = ((), (), s32[]{:S(2)}) async-start(), calls=%async_computation | async-start | bytes 4194304 | tf_op jit(solution)/shard_map/psum | solution.py:77
  11.5 11.1 %copy-start.10 = (s32[512,2]{0,1:T(2,128)S(1)}, s32[512,2]{0,1:T(2,128)}, u32[]{:S(2)}) copy-start(s32[512,2]{0,1:T(2,128)} %param.22) | copy-start | bytes 12292
  16.8 1.3 copy-start.7
  18.1 6.2 %copy-start.2 = (bf16[512,2048]{1,0:T(8,128)(2,1)S(1)}, bf16[512,2048]{1,0:T(8,128)(2,1)}, u32[]{:S(2)}) copy-start(bf16[512,2048]{1,0:T(8,128)(2,1)} %param.18) | copy-start | bytes 6291460
  26.1 8.2 %copy-start.16 = (f32[2048]{0:T(1024)S(1)}, f32[2048]{0:T(1024)}, u32[]{:S(2)}) copy-start(f32[2048]{0:T(1024)} %param.24) | copy-start | bytes 24580
  72.6 7.0 %copy-start.8 = (f32[512,64]{1,0:T(8,128)S(1)}, f32[512,64]{1,0:T(8,128)}, u32[]{:S(2)}) copy-start(f32[512,64]{1,0:T(8,128)} %copy.89) | copy-start | bytes 393220
  75.5 4.1 %copy-start.9 = (f32[512,64]{1,0:T(8,128)S(1)}, f32[512,64]{1,0:T(8,128)}, u32[]{:S(2)}) copy-start(f32[512,64]{1,0:T(8,128)} %copy.90) | copy-start | bytes 393220
  83.6 14.4 %copy-start.11 = (pred[512,16]{1,0:T(8,128)(4,1)S(1)}, pred[512,16]{1,0:T(8,128)(4,1)}, u32[]{:S(2)}) copy-start(pred[512,16]{1,0:T(8,128)(4,1)} %get-tuple-element.16) | copy-start | bytes 24580
  123.6 20.3 %copy-start.12 = (s32[512,2]{0,1:T(2,128)S(1)}, s32[512,2]{0,1:T(2,128)}, u32[]{:S(2)}) copy-start(s32[512,2]{0,1:T(2,128)} %param.23) | copy-start | bytes 12292
  143.8 53.0 %copy-start.14 = (f32[2048]{0:T(1024)S(1)}, f32[2048]{0:T(1024)}, u32[]{:S(2)}) copy-start(f32[2048]{0:T(1024)} %param.29) | copy-start | bytes 24580
  143.8 209.9 %all-reduce.5.cloned.1.call-start = ((), (), s32[]{:S(2)}) async-start(), calls=%async_computation.1 | async-start | bytes 4194304 | tf_op jit(solution)/shard_map/psum | solution.py:84
  194.3 2.5 copy-start.4
  197.9 32.4 %copy-start.5 = (bf16[512,2048]{1,0:T(8,128)(2,1)}, bf16[512,2048]{1,0:T(8,128)(2,1)S(1)}, u32[]{:S(2)}) copy-start(bf16[512,2048]{1,0:T(8,128)(2,1)S(1)} %fusion.14) | copy-start | bytes 6291460
  197.9 32.4 %copy-start.13 = (bf16[2048,8]{0,1:T(8,128)(2,1)S(1)}, bf16[2048,8]{0,1:T(8,128)(2,1)}, u32[]{:S(2)}) copy-start(bf16[2048,8]{0,1:T(8,128)(2,1)} %param.30) | copy-start | bytes 98308
  230.9 6.9 %copy-start.6 = (bf16[512,2048]{1,0:T(8,128)(2,1)S(1)}, bf16[512,2048]{1,0:T(8,128)(2,1)}, u32[]{:S(2)}) copy-start(bf16[512,2048]{1,0:T(8,128)(2,1)} %copy-done.5) | copy-start | bytes 6291460
  237.9 33.8 %copy-start.15 = (s32[2]{0:T(128)S(1)}, s32[2]{0:T(128)}, u32[]{:S(2)}) copy-start(s32[2]{0:T(128)} %iota_add_fusion) | copy-start | bytes 28
  271.8 81.9 %copy-start.3 = (bf16[512,2048]{1,0:T(8,128)(2,1)S(1)}, bf16[512,2048]{1,0:T(8,128)(2,1)}, u32[]{:S(2)}) copy-start(bf16[512,2048]{1,0:T(8,128)(2,1)} %param.18) | copy-start | bytes 6291460
  306.0 52.7 %copy-start.1 = (bf16[2048,8]{0,1:T(8,128)(2,1)S(1)}, bf16[2048,8]{0,1:T(8,128)(2,1)}, u32[]{:S(2)}) copy-start(bf16[2048,8]{0,1:T(8,128)(2,1)} %param.26) | copy-start | bytes 98308
Sparse Core Ops, SparseCore 0:
  144.0 50.2 all-reduce.2
  306.1 47.5 all-reduce.4
where the time goes:
time: 371 us; the launch traced here: 366 us
  matrix products  158 us (43%)
  waiting for transfers between devices  97.2 us (26%)
  local copies, waits for them, and re-layouts  50.8 us (14%)
  other arithmetic  44.8 us (12%)
  between operations  14.9 us (4%)
    psum x1, waiting for transfers between devices, local_step(): att_sum = lax.psum(att_part.astype(jnp.bfloat16), 'tp').astype(jnp.float32)  49.5 us
    psum x1, waiting for transfers between devices, local_step(): mlp_sum = lax.psum(mlp_part.astype(jnp.bfloat16), 'tp').astype(jnp.float32)  47.7 us
    dot_general x1, matrix products, expert_part(): jnp.einsum('bef,efd->bed', activation, w_down, preferred_element_type=jnp...  34.2 us
    dot_general x1, matrix products, expert_part(): jnp.einsum('bd,edf->bef', normed, w_up, preferred_element_type=jnp.float32)  33.8 us
    dot_general x1, matrix products, expert_part(): jnp.einsum('bd,edf->bef', normed, w_gate, preferred_element_type=jnp.floa...  32.4 us
    gather x2, local copies, waits for them, and re-layouts, attention_part(): jnp.take_along_axis(query_all, att_ids[:, :, None], axis=1)  21.2 us
    dot_general x1, matrix products, attention_part(): jnp.einsum('bec,ecd->bed', out_slots, w_out, preferred_element_type=jnp.f...  20.2 us
    gather x10, local copies, waits for them, and re-layouts, route_weights(): jnp.take_along_axis(logits, choice_ids, axis=1)  14.8 us
  transfers between devices with their start and end apart: 2, of which 2 were waited for; matrix products, arithmetic and copies ran while one was open for 0% of the time, Pallas kernels for 0%

commit v1 on v0

v1 whole, which is shorter than its diff:
```python
import functools

import jax
import jax.numpy as jnp
import numpy as np
from jax import lax
from jax.experimental import pallas as pl
from jax.experimental.pallas import tpu as pltpu
from jax.sharding import PartitionSpec as P

NORM_EPS = 1e-6
ROPE_BASE = 10000.0
BF = jnp.bfloat16
F32 = jnp.float32
MESH = pl.DeviceIdType.MESH
VMEM_BYTES = 60 * 1024 * 1024

TOK = 512
HID = 2048
HEADS = 4
HD = 128
SLOTS = 16
ATT_E = 8
FFN = 5632
SUB = 64


def vspec():
    return pl.BlockSpec(memory_space=pltpu.VMEM)


def hspec():
    return pl.BlockSpec(memory_space=pl.ANY)


def dot(a, b):
    return jnp.dot(a, b, preferred_element_type=F32)


def dot_nt(a, b):
    return lax.dot_general(a, b, (((1,), (1,)), ((), ())), preferred_element_type=F32)


def norm_rows(x, gain):
    v = x.astype(F32)
    inv = lax.rsqrt(jnp.mean(v * v, axis=-1, keepdims=True) + NORM_EPS)
    return (v * inv * gain).astype(BF)


def columns_of(rows):
    pad = jnp.zeros((128 - rows.shape[0], TOK), F32)
    return jnp.concatenate([rows.astype(F32), pad], axis=0).T


def pair_gates(logits, id0, id1):
    lane = lax.broadcasted_iota(jnp.int32, logits.shape, 1).astype(F32)
    l0 = jnp.sum(jnp.where(lane == id0, logits, 0.0), axis=1, keepdims=True)
    l1 = jnp.sum(jnp.where(lane == id1, logits, 0.0), axis=1, keepdims=True)
    top = jnp.maximum(l0, l1)
    e0 = jnp.exp(l0 - top)
    e1 = jnp.exp(l1 - top)
    total = e0 + e1
    return e0 / total, e1 / total


def attention_kernel(x_ref, gain_ref, wkv_hbm, router_ref, wq_hbm, kc_hbm, vc_hbm, rows_ref, cos_ref, sin_ref,
                     ko_hbm, vo_hbm, o_ref, meta_ref,
                     h, wkv, wq, cosb, sinb, qf, kvb, qb, q8, kn8, vn8, pos8, o8, kin, vin, kout, vout,
                     wkv_sem, wq_sem, kin_sem, vin_sem, ko_sem, vo_sem):
    ring = wq.shape[0]
    steps = TOK // SUB
    cache_rows = SUB * SLOTS * HEADS

    def cache_rows_at(i):
        return pl.ds(pl.multiple_of(i * cache_rows, cache_rows), cache_rows)

    def wq_copy(e):
        return pltpu.make_async_copy(wq_hbm.at[e], wq.at[e % ring], wq_sem.at[e % ring])

    def in_copies(i):
        s = i % 2
        return (pltpu.make_async_copy(kc_hbm.at[cache_rows_at(i)], kin.at[s], kin_sem.at[s]),
                pltpu.make_async_copy(vc_hbm.at[cache_rows_at(i)], vin.at[s], vin_sem.at[s]))

    def out_copies(i):
        s = i % 2
        return (pltpu.make_async_copy(kout.at[s], ko_hbm.at[cache_rows_at(i)], ko_sem.at[s]),
                pltpu.make_async_copy(vout.at[s], vo_hbm.at[cache_rows_at(i)], vo_sem.at[s]))

    wkv_copy = pltpu.make_async_copy(wkv_hbm, wkv, wkv_sem)
    wkv_copy.start()
    for e in range(ring):
        wq_copy(e).start()
    for i in range(2):
        for c in in_copies(i):
            c.start()

    gain = gain_ref[...]

    def norm_step(i, _):
        r = pl.ds(pl.multiple_of(i * 64, 64), 64)
        h[r, :] = norm_rows(x_ref[r, :], gain)
        return 0

    lax.fori_loop(0, TOK // 64, norm_step, 0)

    cols = columns_of(rows_ref[...])
    id0, id1, pos = cols[:, 0:1], cols[:, 1:2], cols[:, 2:3]
    logits = dot_nt(h[...], router_ref[...])
    g0, g1 = pair_gates(logits, id0, id1)
    lane = lax.broadcasted_iota(jnp.int32, (TOK, 128), 1)
    meta_ref[...] = jnp.where(lane == 0, id0, jnp.where(lane == 1, id1, jnp.where(lane == 2, g0, jnp.where(lane == 3, g1, pos))))

    cb = jnp.zeros((TOK, HD), F32)
    sb = jnp.zeros((TOK, HD), F32)
    for p in range(SLOTS):
        hit = pos == float(p)
        cb = jnp.where(hit, cos_ref[p:p + 1, :], cb)
        sb = jnp.where(hit, sin_ref[p:p + 1, :], sb)
    cosb[...] = cb
    sinb[...] = sb

    def rope(v):
        return v * cosb[...] + pltpu.roll(v, HD // 2, 1) * sinb[...]

    wkv_copy.wait()
    half = HEADS * HD
    kf = dot(h[...], wkv[:, 0:half])
    for n in range(HEADS):
        kvb[:, n * HD:(n + 1) * HD] = rope(kf[:, n * HD:(n + 1) * HD]).astype(BF)
    kvb[:, half:2 * half] = dot(h[...], wkv[:, half:2 * half]).astype(BF)

    def query_step(e, _):
        wq_copy(e).wait()
        ef = e.astype(F32)
        qe = dot(h[...], wq[e % ring])
        m0 = meta_ref[:, 0:1] == ef
        m1 = meta_ref[:, 1:2] == ef
        qf[:, 0:half] = jnp.where(m0, qe, qf[:, 0:half])
        qf[:, half:2 * half] = jnp.where(m1, qe, qf[:, half:2 * half])

        @pl.when(e + ring < ATT_E)
        def _():
            wq_copy(e + ring).start()
        return 0

    lax.fori_loop(0, ATT_E, query_step, 0)
    for n in range(2 * HEADS):
        c = slice(n * HD, (n + 1) * HD)
        qb[:, c] = rope(qf[:, c]).astype(BF)

    group = 4
    rows = group * 2 * HEADS
    lane32 = lax.broadcasted_iota(jnp.int32, (rows, 128), 1)
    row32 = lax.broadcasted_iota(jnp.int32, (rows, 128), 0)
    own_part = ((lane32 // 64) == ((row32 // 8) % 2)) & ((lane32 % 4) == (row32 % 4))
    slot32 = ((lane32 // 4) % 16).astype(F32)
    slot_id = (2 * lax.broadcasted_iota(jnp.int32, (8, 8, 128), 0) + lax.broadcasted_iota(jnp.int32, (8, 8, 128), 1) // 4).astype(F32)
    scale = HD ** -0.5
    upper = row32 < rows // 2

    def cache_step(i, _):
        s = i % 2
        r = pl.ds(pl.multiple_of(i * SUB, SUB), SUB)
        for j in range(2 * HEADS):
            q8[pl.ds(j, SUB, stride=8), :] = qb[r, j * HD:(j + 1) * HD].astype(F32)
            n = j % HEADS
            kn8[pl.ds(j, SUB, stride=8), :] = kvb[r, n * HD:(n + 1) * HD].astype(F32)
            vn8[pl.ds(j, SUB, stride=8), :] = kvb[r, half + n * HD:half + (n + 1) * HD].astype(F32)
            pos8[pl.ds(j, SUB, stride=8), :] = jnp.broadcast_to(meta_ref[r, 4:5], (SUB, 128))

        @pl.when(i >= 2)
        def _():
            for c in out_copies(i - 2):
                c.wait()
        for c in in_copies(i):
            c.wait()

        for part in range(SUB // 32):
            scores = []
            for g in range(8):
                b0 = part * 32 + g * group
                rr = slice(b0 * 64, (b0 + group) * 64)
                r8 = slice(b0 * 8, (b0 + group) * 8)
                hit = slot_id[None] == pos8[r8, :].reshape(group, 1, 8, 128)
                old_k = kin[s, rr, :].astype(F32).reshape(group, 8, 8, 128)
                new_k = jnp.where(hit, kn8[r8, :].reshape(group, 1, 8, 128), old_k).astype(BF).reshape(group * 64, 128)
                kout[s, rr, :] = new_k
                old_v = vin[s, rr, :].astype(F32).reshape(group, 8, 8, 128)
                new_v = jnp.where(hit, vn8[r8, :].reshape(group, 1, 8, 128), old_v).astype(BF).reshape(group * 64, 128)
                vout[s, rr, :] = new_v
                sc = dot_nt(q8[r8, :].astype(BF), new_k)
                scores.append(jnp.concatenate([sc[0:rows // 2, 0:128], sc[rows // 2:, 128:256]], axis=0))
            for g in range(8):
                b0 = part * 32 + g * group
                rr = slice(b0 * 64, (b0 + group) * 64)
                r8 = slice(b0 * 8, (b0 + group) * 8)
                valid = own_part & (slot32 <= pos8[r8, :])
                sc = jnp.where(valid, scores[g] * scale, -1e30)
                ex = jnp.exp(sc - jnp.max(sc, axis=1, keepdims=True))
                w = ex / jnp.sum(ex, axis=1, keepdims=True)
                wide = jnp.concatenate([jnp.where(upper, w, 0.0), jnp.where(upper, 0.0, w)], axis=1).astype(BF)
                o8[r8, :] = dot(wide, vout[s, rr, :])

        for c in out_copies(i):
            c.start()

        @pl.when(i + 2 < steps)
        def _():
            for c in in_copies(i + 2):
                c.start()
        for j in range(2 * HEADS):
            o_ref[r, j * HD:(j + 1) * HD] = o8[pl.ds(j, SUB, stride=8), :].astype(BF)
        return 0

    lax.fori_loop(0, steps, cache_step, 0)
    for i in range(steps - 2, steps):
        for c in out_copies(i):
            c.wait()


def attention_call(x, gain, wkv, router_t, wq, kc, vc, rows, cos_tab, sin_tab):
    ring = 4
    cache_rows = SUB * SLOTS * HEADS
    cache = jax.ShapeDtypeStruct(kc.shape, BF)
    return pl.pallas_call(
        attention_kernel,
        out_shape=(cache, cache, jax.ShapeDtypeStruct((TOK, 2 * HEADS * HD), BF), jax.ShapeDtypeStruct((TOK, 128), F32)),
        in_specs=[vspec(), vspec(), hspec(), vspec(), hspec(), hspec(), hspec(), vspec(), vspec(), vspec()],
        out_specs=(hspec(), hspec(), vspec(), vspec()),
        scratch_shapes=[
            pltpu.VMEM((TOK, HID), BF),
            pltpu.VMEM(wkv.shape, BF),
            pltpu.VMEM((ring,) + wq.shape[1:], BF),
            pltpu.VMEM((TOK, HD), F32), pltpu.VMEM((TOK, HD), F32),
            pltpu.VMEM((TOK, 2 * HEADS * HD), F32),
            pltpu.VMEM((TOK, 2 * HEADS * HD), BF),
            pltpu.VMEM((TOK, 2 * HEADS * HD), BF),
            pltpu.VMEM((SUB * 8, 128), F32), pltpu.VMEM((SUB * 8, 128), F32), pltpu.VMEM((SUB * 8, 128), F32),
            pltpu.VMEM((SUB * 8, 128), F32), pltpu.VMEM((SUB * 8, 128), F32),
            pltpu.VMEM((2, cache_rows, HD), BF), pltpu.VMEM((2, cache_rows, HD), BF),
            pltpu.VMEM((2, cache_rows, HD), BF), pltpu.VMEM((2, cache_rows, HD), BF),
            pltpu.SemaphoreType.DMA, pltpu.SemaphoreType.DMA((ring,)),
            pltpu.SemaphoreType.DMA((2,)), pltpu.SemaphoreType.DMA((2,)),
            pltpu.SemaphoreType.DMA((2,)), pltpu.SemaphoreType.DMA((2,)),
        ],
        compiler_params=pltpu.CompilerParams(vmem_limit_bytes=VMEM_BYTES),
        name="attention",
    )(x, gain, wkv, router_t, wq, kc, vc, rows, cos_tab, sin_tab)


HALF = TOK // 2


class PairSum:
    def __init__(self, part, r1, cs, r2, fin, r3, sems):
        self.part, self.r1, self.cs, self.r2, self.fin, self.r3 = part, r1, cs, r2, fin, r3
        self.sems = sems
        me = lax.axis_index("tp")
        chip, core = me // 2, me % 2
        self.sib = chip * 2 + (1 - core)
        self.peer = (1 - chip) * 2 + core
        self.own = pl.ds(pl.multiple_of(core * HALF, HALF), HALF)
        self.other = pl.ds(pl.multiple_of((1 - core) * HALF, HALF), HALF)

    def greet(self):
        barrier = pltpu.get_barrier_semaphore()
        for d in (self.sib, self.peer):
            pl.semaphore_signal(barrier, inc=1, device_id={"tp": d}, device_id_type=MESH)
        pl.semaphore_wait(barrier, 2)

    def copy(self, stage, j):
        src, dst, to = ((self.part.at[j, self.other], self.r1.at[j], self.sib),
                        (self.cs.at[j], self.r2.at[j], self.peer),
                        (self.fin.at[j], self.r3.at[j], self.sib))[stage]
        return pltpu.make_async_remote_copy(src, dst, self.sems.at[0, stage, j], self.sems.at[1, stage, j],
                                            device_id={"tp": to}, device_id_type=MESH)

    def first(self, j):
        self.copy(0, j).start()

    def second(self, j):
        self.copy(0, j).wait()
        self.cs[j] = (self.part[j, self.own].astype(F32) + self.r1[j].astype(F32)).astype(BF)
        self.copy(1, j).start()

    def third(self, j, base_ref, cols):
        self.copy(1, j).wait()
        both = self.cs[j].astype(F32) + self.r2[j].astype(F32)
        self.fin[j] = (base_ref[self.own, cols].astype(F32) + both).astype(BF)
        self.copy(2, j).start()

    def last(self, j, out_ref, cols):
        self.copy(2, j).wait()
        out_ref[self.own, cols] = self.fin[j]
        out_ref[self.other, cols] = self.r3[j]


def pair_scratch(chunks, width):
    return [
        pltpu.VMEM((chunks, TOK, width), BF),
        pltpu.VMEM((chunks, HALF, width), BF), pltpu.VMEM((chunks, HALF, width), BF),
        pltpu.VMEM((chunks, HALF, width), BF), pltpu.VMEM((chunks, HALF, width), BF),
        pltpu.VMEM((chunks, HALF, width), BF),
        pltpu.SemaphoreType.DMA((2, 3, chunks)),
    ]


def project_kernel(x_ref, o_ref, meta_ref, wo_hbm, xm_ref, wo, oe, gb, acc, wo_sem, part, r1, cs, r2, fin, r3, sems):
    chunks, width = part.shape[0], part.shape[2]
    ring = wo.shape[0]
    half = HEADS * HD

    def wo_copy(j):
        return pltpu.make_async_copy(wo_hbm.at[:, :, pl.ds(pl.multiple_of(j * width, width), width)], wo.at[j % ring], wo_sem.at[j % ring])

    for j in range(ring):
        wo_copy(j).start()
    net = PairSum(part, r1, cs, r2, fin, r3, sems)
    net.greet()
    for e in range(ATT_E):
        m0 = meta_ref[:, 0:1] == float(e)
        m1 = meta_ref[:, 1:2] == float(e)
        first = jnp.where(m0, o_ref[:, 0:half].astype(F32), 0.0)
        oe[e] = jnp.where(m1, o_ref[:, half:2 * half].astype(F32), first).astype(BF)
        gate = jnp.where(m0, meta_ref[:, 2:3], jnp.where(m1, meta_ref[:, 3:4], 0.0))
        gb[e] = jnp.broadcast_to(gate, (TOK, 128))

    def chunk_step(j, _):
        wo_copy(j).wait()
        slot = j % ring

        def expert_step(e, _):
            prod = dot(oe[e], wo[slot, e])
            gate = gb[e]
            for n in range(width // 128):
                c = slice(n * 128, (n + 1) * 128)
                acc[:, c] = jnp.where(e == 0, 0.0, acc[:, c]) + gate * prod[:, c]
            return 0

        lax.fori_loop(0, ATT_E, expert_step, 0)
        part[j] = acc[...].astype(BF)

        @pl.when(j + ring < chunks)
        def _():
            wo_copy(j + ring).start()
        net.first(j)
        net.second(j)
        return 0

    lax.fori_loop(0, chunks, chunk_step, 0)
    for j in range(chunks):
        net.third(j, x_ref, slice(j * width, (j + 1) * width))
        if j >= 1:
            net.last(j - 1, xm_ref, slice((j - 1) * width, j * width))
    net.last(chunks - 1, xm_ref, slice((chunks - 1) * width, chunks * width))


def project_call(x, o, meta, wo):
    chunks = 4
    width = HID // chunks
    ring = 2
    return pl.pallas_call(
        project_kernel,
        out_shape=jax.ShapeDtypeStruct((TOK, HID), BF),
        in_specs=[vspec(), vspec(), vspec(), hspec()],
        out_specs=vspec(),
        scratch_shapes=[
            pltpu.VMEM((ring, ATT_E, HEADS * HD, width), BF),
            pltpu.VMEM((ATT_E, TOK, HEADS * HD), BF),
            pltpu.VMEM((ATT_E, TOK, 128), F32),
            pltpu.VMEM((TOK, width), F32),
            pltpu.SemaphoreType.DMA((ring,)),
        ] + pair_scratch(chunks, width),
        compiler_params=pltpu.CompilerParams(vmem_limit_bytes=VMEM_BYTES, collective_id=0, has_side_effects=True),
        name="project_sum",
    )(x, o, meta, wo)


FB = 512
NF = FFN // FB


def gate_up_kernel(xm_ref, gain_ref, router_ref, ids_ref, wg_hbm, wu_hbm, a_hbm, gates_ref,
                   u, pick, spread, xc, wg, wu, ab, count, wg_sem, wu_sem, a_sem):
    ring = wg.shape[0]
    steps = 2 * NF
    first_id = lax.axis_index("tp") * 2

    def in_copies(t):
        f = pl.ds(pl.multiple_of((t % NF) * FB, FB), FB)
        s = t % ring
        return (pltpu.make_async_copy(wg_hbm.at[t // NF, :, f], wg.at[s], wg_sem.at[s]),
                pltpu.make_async_copy(wu_hbm.at[t // NF, :, f], wu.at[s], wu_sem.at[s]))

    def out_copy(t):
        f = pl.ds(pl.multiple_of((t % NF) * FB, FB), FB)
        return pltpu.make_async_copy(ab.at[t % 2], a_hbm.at[t // NF, :, f], a_sem.at[t % 2])

    for t in range(ring):
        for c in in_copies(t):
            c.start()

    gain = gain_ref[...]

    def norm_step(i, _):
        r = pl.ds(pl.multiple_of(i * 64, 64), 64)
        u[r, :] = norm_rows(xm_ref[r, :], gain)
        return 0

    lax.fori_loop(0, TOK // 64, norm_step, 0)
    cols = columns_of(ids_ref[...])
    id0, id1 = cols[:, 0:1], cols[:, 1:2]
    logits = dot_nt(u[...], router_ref[...])
    g0, g1 = pair_gates(logits, id0, id1)
    lane = lax.broadcasted_iota(jnp.int32, (TOK, 128), 1)
    mine = (lane + first_id).astype(F32)
    gates_ref[...] = jnp.where(mine == id0, g0, jnp.where(mine == id1, g1, 0.0))

    def expert_rows(e):
        target = first_id + e
        hit = ((ids_ref[0:1, :] == target) | (ids_ref[1:2, :] == target)).astype(F32)
        before = lax.broadcasted_iota(jnp.int32, (TOK, TOK), 0) < lax.broadcasted_iota(jnp.int32, (TOK, TOK), 1)
        hit8 = jnp.broadcast_to(hit, (8, TOK))
        rank = dot(hit8.astype(BF), before.astype(F32).astype(BF))[0:1, :]
        place = jnp.where(hit > 0.5, rank, -1.0)
        row = lax.broadcasted_iota(jnp.int32, (TOK, TOK), 0).astype(F32)
        sel = (row == place).astype(F32)
        pick[...] = sel.astype(BF)
        spread[...] = sel.T.astype(BF)
        xc[...] = dot(pick[...], u[...]).astype(BF)
        count[0] = (jnp.sum(hit).astype(jnp.int32) + 127) // 128

    def block_step(t, _):
        @pl.when(t % NF == 0)
        def _():
            expert_rows(t // NF)
        s = t % ring
        for c in in_copies(t):
            c.wait()

        @pl.when(t >= 2)
        def _():
            out_copy(t - 2).wait()
        blocks = count[0]

        def run(m):
            g = dot(xc[0:m, :], wg[s])
            up = dot(xc[0:m, :], wu[s])
            act = (jax.nn.silu(g) * up).astype(BF)
            ab[t % 2] = dot(spread[:, 0:m], act).astype(BF)

        for n in range(1, 5):
            @pl.when((blocks == n) if n > 1 else (blocks <= 1))
            def _(n=n):
                run(128 * n)
        out_copy(t).start()

        @pl.when(t + ring < steps)
        def _():
            for c in in_copies(t + ring):
                c.start()
        return 0

    lax.fori_loop(0, steps, block_step, 0)
    for t in range(steps - 2, steps):
        out_copy(t).wait()


def gate_up_call(xm, gain, router_t, ids, wg, wu):
    ring = 4
    return pl.pallas_call(
        gate_up_kernel,
        out_shape=(jax.ShapeDtypeStruct((2, TOK, FFN), BF), jax.ShapeDtypeStruct((TOK, 128), F32)),
        in_specs=[vspec(), vspec(), vspec(), vspec(), hspec(), hspec()],
        out_specs=(hspec(), vspec()),
        scratch_shapes=[
            pltpu.VMEM((TOK, HID), BF), pltpu.VMEM((TOK, TOK), BF), pltpu.VMEM((TOK, TOK), BF), pltpu.VMEM((TOK, HID), BF),
            pltpu.VMEM((ring, HID, FB), BF), pltpu.VMEM((ring, HID, FB), BF), pltpu.VMEM((2, TOK, FB), BF),
            pltpu.SMEM((1,), jnp.int32),
            pltpu.SemaphoreType.DMA((ring,)), pltpu.SemaphoreType.DMA((ring,)), pltpu.SemaphoreType.DMA((2,)),
        ],
        compiler_params=pltpu.CompilerParams(vmem_limit_bytes=VMEM_BYTES),
        name="gate_up",
    )(xm, gain, router_t, ids, wg, wu)


def down_kernel(xm_ref, a_hbm, gates_ref, wd_hbm, out_ref, a, wd, acc, a_sem, wd_sem, part, r1, cs, r2, fin, r3, sems):
    chunks, width = part.shape[0], part.shape[2]
    ring = wd.shape[0]
    total = 2 * chunks

    def wd_copy(t):
        cols = pl.ds(pl.multiple_of((t // 2) * width, width), width)
        return pltpu.make_async_copy(wd_hbm.at[t % 2, :, cols], wd.at[t % ring], wd_sem.at[t % ring])

    for e in range(2):
        pltpu.make_async_copy(a_hbm.at[e], a.at[e], a_sem.at[e]).start()
        wd_copy(e).start()
    for t in range(2, ring):
        wd_copy(t).start()
    net = PairSum(part, r1, cs, r2, fin, r3, sems)
    net.greet()
    for e in range(2):
        pltpu.make_async_copy(a_hbm.at[e], a.at[e], a_sem.at[e]).wait()

    def chunk_step(j, _):
        for e in range(2):
            t = 2 * j + e
            wd_copy(t).wait()
            prod = dot(a[e], wd[t % ring]) * gates_ref[:, e:e + 1]
            if e == 0:
                acc[...] = prod
            else:
                part[j] = (acc[...] + prod).astype(BF)

            @pl.when(t + ring < total)
            def _():
                wd_copy(t + ring).start()
        net.first(j)

        @pl.when(j >= 1)
        def _():
            net.second(j - 1)
        return 0

    lax.fori_loop(0, chunks, chunk_step, 0)
    net.second(chunks - 1)
    for j in range(chunks):
        net.third(j, xm_ref, slice(j * width, (j + 1) * width))
        if j >= 1:
            net.last(j - 1, out_ref, slice((j - 1) * width, j * width))
    net.last(chunks - 1, out_ref, slice((chunks - 1) * width, chunks * width))


def down_call(xm, a, gates, wd):
    chunks = 4
    width = HID // chunks
    ring = 3
    return pl.pallas_call(
        down_kernel,
        out_shape=jax.ShapeDtypeStruct((TOK, HID), BF),
        in_specs=[vspec(), hspec(), vspec(), hspec()],
        out_specs=vspec(),
        scratch_shapes=[
            pltpu.VMEM((2, TOK, FFN), BF),
            pltpu.VMEM((ring, FFN, width), BF),
            pltpu.VMEM((TOK, width), F32),
            pltpu.SemaphoreType.DMA((2,)), pltpu.SemaphoreType.DMA((ring,)),
        ] + pair_scratch(chunks, width),
        compiler_params=pltpu.CompilerParams(vmem_limit_bytes=VMEM_BYTES, collective_id=1, has_side_effects=True),
        name="down_sum",
    )(xm, a, gates, wd)


def rope_tables():
    inv_freq = np.power(np.float64(ROPE_BASE), -(np.arange(HD // 2) * 2.0 / HD))
    angle = (np.arange(SLOTS, dtype=np.float32)[:, None] * inv_freq.astype(np.float32)[None, :]).astype(np.float64)
    cos = np.cos(angle).astype(np.float32)
    sin = np.sin(angle).astype(np.float32)
    return np.concatenate([cos, cos], axis=1), np.concatenate([-sin, sin], axis=1)


def solution(mesh):
    cos_tab, sin_tab = rope_tables()

    def local_step(x, k_cache, v_cache, positions, att_ids, mlp_ids, norm_att, w_kv, router_att, w_query, w_out, norm_mlp, router_mlp, w_gate, w_up, w_down):
        flat = (TOK * SLOTS * HEADS, HD)
        wkv = w_kv.reshape(HID, HEADS, 2, HD).transpose(0, 2, 1, 3).reshape(HID, 2 * HEADS * HD)
        rows = jnp.concatenate([att_ids.T, positions[None, :]], axis=0)
        k_out, v_out, o, meta = attention_call(
            x, norm_att[None, :], wkv, router_att.T, w_query, k_cache.reshape(flat), v_cache.reshape(flat), rows,
            jnp.asarray(cos_tab), jnp.asarray(sin_tab))
        xm = project_call(x, o, meta, w_out)
        a, gates = gate_up_call(xm, norm_mlp[None, :], router_mlp.T, mlp_ids.T, w_gate, w_up)
        x_out = down_call(xm, a, gates, w_down)
        return x_out, k_out.reshape(k_cache.shape), v_out.reshape(v_cache.shape)

    token_spec = P('dp', None)
    cache_spec = P('dp', None, 'tp', None)
    expert_spec = P('tp', None, None)
    in_specs = (token_spec, cache_spec, cache_spec, P('dp'), token_spec, token_spec, P(), P(None, 'tp', None), P(), P(None, None, 'tp'), P(None, 'tp', None), P(), P(), expert_spec, expert_spec, expert_spec)
    out_specs = (token_spec, cache_spec, cache_spec)
    return jax.shard_map(local_step, mesh=mesh, in_specs=in_specs, out_specs=out_specs, check_vma=False)
```

time: 371 us -> 183 us (0.49); the launches traced: 366 us -> 182 us
  Pallas kernels: 0 us -> 169 us
  matrix products: 158 us -> 0 us
  waiting for transfers between devices: 97.2 us -> 0 us
  other arithmetic: 44.8 us -> 1.31 us
  local copies, waits for them, and re-layouts: 50.8 us -> 10.8 us
  between operations: 14.9 us -> 0.66 us
    pallas_call x0 -> x4, Pallas kernels: none -> 169 us  [the longest x1 59 us: down_call(): pl.pallas_call(down_kernel, out_shape=jax.ShapeDtypeStruct((TOK, HID), BF...]
    dot_general x10 -> x0, matrix products: 158 us -> none  [the longest x1 34.2 us: expert_part(): jnp.einsum('bef,efd->bed', activation, w_down, preferred_element_type=jnp...]
    psum x2 -> x0, waiting for transfers between devices: 97.2 us -> none  [the longest x1 49.5 us: local_step(): att_sum = lax.psum(att_part.astype(jnp.bfloat16), 'tp').astype(jnp.float32)]
    gather x12 -> x0, local copies, waits for them, and re-layouts: 36 us -> none  [the longest x2 21.2 us: attention_part(): jnp.take_along_axis(query_all, att_ids[:, :, None], axis=1)]
    select_n x2 -> x0, other arithmetic: 18.4 us -> none  [the longest x1 14.4 us: attention_part(): keys_all = jnp.where(at_slot, key_new[:, None, :, :], k_cache)]
    dot_general x1 -> x0, local copies, waits for them, and re-layouts: 8.25 us -> none  [attention_part(): jnp.einsum('bd,edc->bec', hidden, w_query, preferred_element_type=jnp.flo...]
    reshape x0 -> x1, local copies, waits for them, and re-layouts: none -> 7.69 us  [local_step(): w_kv.reshape(HID, HEADS, 2, HD).transpose(0, 2, 1, 3)]
    sub x1 -> x0, other arithmetic: 6.93 us -> none  [attention_part(): jax.nn.softmax(jnp.where(visible, scores, -1e+30), axis=-1)]
  transfers between devices with their start and end apart: 2 -> 0, of which waited for: 2 -> 0; matrix products, arithmetic and copies ran while one was open for 0% -> 0% of each run, Pallas kernels for 0% -> 0%
where the time goes in v1:
time: 183 us; the launch traced here: 182 us
  Pallas kernels  169 us (92%)
  local copies, waits for them, and re-layouts  10.8 us (6%)
    pallas_call x1, Pallas kernels, down_call(): pl.pallas_call(down_kernel, out_shape=jax.ShapeDtypeStruct((TOK, HID), BF...  59 us
    pallas_call x1, Pallas kernels, project_call(): pl.pallas_call(project_kernel, out_shape=jax.ShapeDtypeStruct((TOK, HID),...  40.1 us
    pallas_call x1, Pallas kernels, gate_up_call(): pl.pallas_call(gate_up_kernel, out_shape=(jax.ShapeDtypeStruct((2, TOK, F...  36.3 us
    pallas_call x1, Pallas kernels, attention_call(): pl.pallas_call(attention_kernel, out_shape=(cache, cache, jax.ShapeDtypeS...  33.7 us
    reshape x1, local copies, waits for them, and re-layouts, local_step(): w_kv.reshape(HID, HEADS, 2, HD).transpose(0, 2, 1, 3)  7.69 us

profile of v1, /device:TPU:0, one launch (start us, length us, event | category | flops | bytes accessed | tf_op | source)
XLA Modules:
  0.0 181.9 jit_solution(1973031785575246963)
XLA Ops:
  0.6 1.3 pad_add_fusion.rows_ref
  1.9 7.7 %reshape.25.wkv_hbm = bf16[2048,1024]{1,0:T(8,128)(2,1)} reshape(bf16[2048,2,4,128]{3,2,1,0:T(4,128)(2,1)} %bitcast.16) | data formatting | bytes 8388608 | tf_op jit(solution)/shard_map/reshape | solution.py:569
  9.6 33.7 %attention.1 = (bf16[32768,128]{1,0:T(8,128)(2,1)}, bf16[32768,128]{1,0:T(8,128)(2,1)}, bf16[512,1024]{1,0:T(8,128)(2,1)}, f32[512,128]{1,0:T(8,128)}) custom-call(bf16[512,2048]{1,0:T(8,128)(2,1)} %x_ref.3, f32[1,2048]{1,0:T(1,128)} %bitcast.19, bf16[2048,1024]{1,0:T(8,128)(2,1)} %reshape.25.wkv_hbm, bf16[8,2048]{1,0:T(8,128)(2,1)} %bitcast.17, ...), custom_call_target="tpu_custom_call" | custom-call | tf_op jit(solution)/shard_map/attention/pallas_call | solution.py:226
  43.3 40.1 %project_sum.1.xm_ref = bf16[512,2048]{1,0:T(8,128)(2,1)} custom-call(bf16[512,2048]{1,0:T(8,128)(2,1)} %x_ref.3, bf16[512,1024]{1,0:T(8,128)(2,1)} %get-tuple-element.9.o_ref, f32[512,128]{1,0:T(8,128)} %get-tuple-element.10.meta_ref, bf16[8,512,2048]{2,1,0:T(8,128)(2,1)} %wo_hbm.1), custom_call_target="tpu_custom_call" | custom-call | tf_op jit(solution)/shard_map/project_sum/pallas_call | solution.py:363
  83.4 36.3 %gate_up.1 = (bf16[2,512,5632]{2,1,0:T(8,128)(2,1)}, f32[512,128]{1,0:T(8,128)}) custom-call(bf16[512,2048]{1,0:T(8,128)(2,1)} %project_sum.1.xm_ref, f32[1,2048]{1,0:T(1,128)} %bitcast.20, bf16[8,2048]{1,0:T(8,128)(2,1)} %bitcast.18, s32[2,512]{1,0:T(2,128)} %bitcast.21, bf16[2,2048,5632]{2,1,0:T(8,128)(2,1)} %wg_hbm.1, bf16[2,2048,5632]{2,1,0:T(8,128)(2,1)} %wu_hbm.1), custom_call_target="tpu_custom_call" | custom-call | tf_op jit(solution)/shard_map/gate_up/pallas_call | solution.py:472
  119.7 59.0 %down_sum.1 = bf16[512,2048]{1,0:T(8,128)(2,1)} custom-call(bf16[512,2048]{1,0:T(8,128)(2,1)} %project_sum.1.xm_ref, bf16[2,512,5632]{2,1,0:T(8,128)(2,1)} %get-tuple-element.11.a_hbm, f32[512,128]{1,0:T(8,128)} %get-tuple-element.12.gates_ref, bf16[2,5632,2048]{2,1,0:T(8,128)(2,1)} %wd_hbm.1), custom_call_target="tpu_custom_call" | custom-call | tf_op jit(solution)/shard_map/down_sum/pallas_call | solution.py:540
  178.7 3.2 %copy.23 = bf16[512,2048]{1,0:T(8,128)(2,1)} copy(bf16[512,2048]{1,0:T(8,128)(2,1)} %down_sum.1) | data formatting | bytes 4194304

commit v2 on v1

--- a/solution.py
+++ b/solution.py
@@ -13,7 +13,7 @@
 BF = jnp.bfloat16
 F32 = jnp.float32
 MESH = pl.DeviceIdType.MESH
-VMEM_BYTES = 60 * 1024 * 1024
+VMEM_BYTES = 62 * 1024 * 1024
 
 TOK = 512
 HID = 2048
@@ -63,9 +63,9 @@
     return e0 / total, e1 / total
 
 
-def attention_kernel(x_ref, gain_ref, wkv_hbm, router_ref, wq_hbm, kc_hbm, vc_hbm, rows_ref, cos_ref, sin_ref,
+def attention_kernel(x_ref, gain_ref, wkv_hbm, router_ref, wq_hbm, kc_hbm, vc_hbm, ids_ref, pos_ref, cos_ref, sin_ref,
                      ko_hbm, vo_hbm, o_ref, meta_ref,
-                     h, wkv, wq, cosb, sinb, qf, kvb, qb, q8, kn8, vn8, pos8, o8, kin, vin, kout, vout,
+                     h, wkv_raw, wkv_wide, wkv, wq, cosb, sinb, qf, kvb, qb, q8, kn8, vn8, pos8, o8, kin, vin, kout, vout,
                      wkv_sem, wq_sem, kin_sem, vin_sem, ko_sem, vo_sem):
     ring = wq.shape[0]
     steps = TOK // SUB
@@ -87,7 +87,7 @@
         return (pltpu.make_async_copy(kout.at[s], ko_hbm.at[cache_rows_at(i)], ko_sem.at[s]),
                 pltpu.make_async_copy(vout.at[s], vo_hbm.at[cache_rows_at(i)], vo_sem.at[s]))
 
-    wkv_copy = pltpu.make_async_copy(wkv_hbm, wkv, wkv_sem)
+    wkv_copy = pltpu.make_async_copy(wkv_hbm, wkv_raw, wkv_sem)
     wkv_copy.start()
     for e in range(ring):
         wq_copy(e).start()
@@ -104,7 +104,7 @@
 
     lax.fori_loop(0, TOK // 64, norm_step, 0)
 
-    cols = columns_of(rows_ref[...])
+    cols = columns_of(jnp.concatenate([ids_ref[...], pos_ref[...]], axis=0))
     id0, id1, pos = cols[:, 0:1], cols[:, 1:2], cols[:, 2:3]
     logits = dot_nt(h[...], router_ref[...])
     g0, g1 = pair_gates(logits, id0, id1)
@@ -125,6 +125,15 @@
 
     wkv_copy.wait()
     half = HEADS * HD
+    deep = wkv_wide.shape[0] // 8
+
+    def relayout_step(i, _):
+        wkv_wide[...] = wkv_raw[pl.ds(pl.multiple_of(i * deep * 8, deep * 8), deep * 8), :].astype(F32)
+        for j in range(8):
+            wkv[pl.ds(pl.multiple_of(i * deep, deep), deep), j * HD:(j + 1) * HD] = wkv_wide[pl.ds(j, deep, stride=8), :].astype(BF)
+        return 0
+
+    lax.fori_loop(0, HID // deep, relayout_step, 0)
     kf = dot(h[...], wkv[:, 0:half])
     for n in range(HEADS):
         kvb[:, n * HD:(n + 1) * HD] = rope(kf[:, n * HD:(n + 1) * HD]).astype(BF)
@@ -219,18 +228,18 @@
             c.wait()
 
 
-def attention_call(x, gain, wkv, router_t, wq, kc, vc, rows, cos_tab, sin_tab):
+def attention_call(x, gain, wkv, router_t, wq, kc, vc, ids, pos, cos_tab, sin_tab):
     ring = 4
     cache_rows = SUB * SLOTS * HEADS
     cache = jax.ShapeDtypeStruct(kc.shape, BF)
     return pl.pallas_call(
         attention_kernel,
         out_shape=(cache, cache, jax.ShapeDtypeStruct((TOK, 2 * HEADS * HD), BF), jax.ShapeDtypeStruct((TOK, 128), F32)),
-        in_specs=[vspec(), vspec(), hspec(), vspec(), hspec(), hspec(), hspec(), vspec(), vspec(), vspec()],
+        in_specs=[vspec(), vspec(), hspec(), vspec(), hspec(), hspec(), hspec(), vspec(), vspec(), vspec(), vspec()],
         out_specs=(hspec(), hspec(), vspec(), vspec()),
         scratch_shapes=[
             pltpu.VMEM((TOK, HID), BF),
-            pltpu.VMEM(wkv.shape, BF),
+            pltpu.VMEM(wkv.shape, BF), pltpu.VMEM((2048, HD), F32), pltpu.VMEM((HID, 2 * HEADS * HD), BF),
             pltpu.VMEM((ring,) + wq.shape[1:], BF),
             pltpu.VMEM((TOK, HD), F32), pltpu.VMEM((TOK, HD), F32),
             pltpu.VMEM((TOK, 2 * HEADS * HD), F32),
@@ -246,16 +255,17 @@
         ],
         compiler_params=pltpu.CompilerParams(vmem_limit_bytes=VMEM_BYTES),
         name="attention",
-    )(x, gain, wkv, router_t, wq, kc, vc, rows, cos_tab, sin_tab)
+    )(x, gain, wkv, router_t, wq, kc, vc, ids, pos, cos_tab, sin_tab)
 
 
 HALF = TOK // 2
 
 
 class PairSum:
-    def __init__(self, part, r1, cs, r2, fin, r3, sems):
-        self.part, self.r1, self.cs, self.r2, self.fin, self.r3 = part, r1, cs, r2, fin, r3
+    def __init__(self, part_at, r1, cs, r2, fin, r3, sems):
+        self.part_at, self.r1, self.cs, self.r2, self.fin, self.r3 = part_at, r1, cs, r2, fin, r3
         self.sems = sems
+        self.width = r1.shape[2]
         me = lax.axis_index("tp")
         chip, core = me // 2, me % 2
         self.sib = chip * 2 + (1 - core)
@@ -269,8 +279,11 @@
             pl.semaphore_signal(barrier, inc=1, device_id={"tp": d}, device_id_type=MESH)
         pl.semaphore_wait(barrier, 2)
 
+    def cols(self, j):
+        return pl.ds(pl.multiple_of(j * self.width, self.width), self.width)
+
     def copy(self, stage, j):
-        src, dst, to = ((self.part.at[j, self.other], self.r1.at[j], self.sib),
+        src, dst, to = ((self.part_at(j, self.other), self.r1.at[j], self.sib),
                         (self.cs.at[j], self.r2.at[j], self.peer),
                         (self.fin.at[j], self.r3.at[j], self.sib))[stage]
         return pltpu.make_async_remote_copy(src, dst, self.sems.at[0, stage, j], self.sems.at[1, stage, j],
@@ -281,32 +294,38 @@
 
     def second(self, j):
         self.copy(0, j).wait()
-        self.cs[j] = (self.part[j, self.own].astype(F32) + self.r1[j].astype(F32)).astype(BF)
+        self.cs[j] = (self.part_at(j, self.own)[...].astype(F32) + self.r1[j].astype(F32)).astype(BF)
         self.copy(1, j).start()
 
-    def third(self, j, base_ref, cols):
+    def third(self, j, base_ref):
         self.copy(1, j).wait()
         both = self.cs[j].astype(F32) + self.r2[j].astype(F32)
-        self.fin[j] = (base_ref[self.own, cols].astype(F32) + both).astype(BF)
+        self.fin[j] = (base_ref[self.own, self.cols(j)].astype(F32) + both).astype(BF)
         self.copy(2, j).start()
 
-    def last(self, j, out_ref, cols):
+    def last(self, j, out_ref):
         self.copy(2, j).wait()
-        out_ref[self.own, cols] = self.fin[j]
-        out_ref[self.other, cols] = self.r3[j]
+        out_ref[self.own, self.cols(j)] = self.fin[j]
+        out_ref[self.other, self.cols(j)] = self.r3[j]
+
+    def finish(self, chunks, base_ref, out_ref):
+        def step(j, _):
+            self.third(j, base_ref)
+
+            @pl.when(j >= 1)
+            def _():
+                self.last(j - 1, out_ref)
+            return 0
+
+        lax.fori_loop(0, chunks, step, 0)
+        self.last(chunks - 1, out_ref)
 
 
 def pair_scratch(chunks, width):
-    return [
-        pltpu.VMEM((chunks, TOK, width), BF),
-        pltpu.VMEM((chunks, HALF, width), BF), pltpu.VMEM((chunks, HALF, width), BF),
-        pltpu.VMEM((chunks, HALF, width), BF), pltpu.VMEM((chunks, HALF, width), BF),
-        pltpu.VMEM((chunks, HALF, width), BF),
-        pltpu.SemaphoreType.DMA((2, 3, chunks)),
-    ]
-
-
-def project_kernel(x_ref, o_ref, meta_ref, wo_hbm, xm_ref, wo, oe, gb, acc, wo_sem, part, r1, cs, r2, fin, r3, sems):
+    return [pltpu.VMEM((chunks, HALF, width), BF)] * 5 + [pltpu.SemaphoreType.DMA((2, 3, chunks))]
+
+
+def project_kernel(x_hbm, o_ref, meta_ref, wo_hbm, xm_ref, xv, wo, oe, gb, acc, x_sem, wo_sem, part, r1, cs, r2, fin, r3, sems):
     chunks, width = part.shape[0], part.shape[2]
     ring = wo.shape[0]
     half = HEADS * HD
@@ -316,13 +335,18 @@
 
     for j in range(ring):
         wo_copy(j).start()
-    net = PairSum(part, r1, cs, r2, fin, r3, sems)
+    x_copy = pltpu.make_async_copy(x_hbm, xv, x_sem)
+    x_copy.start()
+    net = PairSum(lambda j, rows: part.at[j, rows], r1, cs, r2, fin, r3, sems)
     net.greet()
     for e in range(ATT_E):
         m0 = meta_ref[:, 0:1] == float(e)
         m1 = meta_ref[:, 1:2] == float(e)
-        first = jnp.where(m0, o_ref[:, 0:half].astype(F32), 0.0)
-        oe[e] = jnp.where(m1, o_ref[:, half:2 * half].astype(F32), first).astype(BF)
+        f0 = jnp.broadcast_to(jnp.where(m0, 1.0, 0.0), (TOK, 128)).astype(BF)
+        f1 = jnp.broadcast_to(jnp.where(m1, 1.0, 0.0), (TOK, 128)).astype(BF)
+        for n in range(HEADS):
+            c = slice(n * HD, (n + 1) * HD)
+            oe[e, :, c] = o_ref[:, c] * f0 + o_ref[:, half + n * HD:half + (n + 1) * HD] * f1
         gate = jnp.where(m0, meta_ref[:, 2:3], jnp.where(m1, meta_ref[:, 3:4], 0.0))
         gb[e] = jnp.broadcast_to(gate, (TOK, 128))
 
@@ -345,32 +369,39 @@
         def _():
             wo_copy(j + ring).start()
         net.first(j)
-        net.second(j)
+
+        @pl.when(j == 0)
+        def _():
+            net.second(j)
+
+        @pl.when(j >= 2)
+        def _():
+            net.second(j - 1)
         return 0
 
     lax.fori_loop(0, chunks, chunk_step, 0)
-    for j in range(chunks):
-        net.third(j, x_ref, slice(j * width, (j + 1) * width))
-        if j >= 1:
-            net.last(j - 1, xm_ref, slice((j - 1) * width, j * width))
-    net.last(chunks - 1, xm_ref, slice((chunks - 1) * width, chunks * width))
+    net.second(chunks - 1)
+    x_copy.wait()
+    net.finish(chunks, xv, xm_ref)
 
 
 def project_call(x, o, meta, wo):
-    chunks = 4
+    chunks = 8
     width = HID // chunks
-    ring = 2
+    ring = 3
     return pl.pallas_call(
         project_kernel,
         out_shape=jax.ShapeDtypeStruct((TOK, HID), BF),
-        in_specs=[vspec(), vspec(), vspec(), hspec()],
+        in_specs=[hspec(), vspec(), vspec(), hspec()],
         out_specs=vspec(),
         scratch_shapes=[
+            pltpu.VMEM((TOK, HID), BF),
             pltpu.VMEM((ring, ATT_E, HEADS * HD, width), BF),
             pltpu.VMEM((ATT_E, TOK, HEADS * HD), BF),
             pltpu.VMEM((ATT_E, TOK, 128), F32),
             pltpu.VMEM((TOK, width), F32),
-            pltpu.SemaphoreType.DMA((ring,)),
+            pltpu.SemaphoreType.DMA, pltpu.SemaphoreType.DMA((ring,)),
+            pltpu.VMEM((chunks, TOK, width), BF),
         ] + pair_scratch(chunks, width),
         compiler_params=pltpu.CompilerParams(vmem_limit_bytes=VMEM_BYTES, collective_id=0, has_side_effects=True),
         name="project_sum",
@@ -379,12 +410,16 @@
 
 FB = 512
 NF = FFN // FB
-
-
-def gate_up_kernel(xm_ref, gain_ref, router_ref, ids_ref, wg_hbm, wu_hbm, a_hbm, gates_ref,
-                   u, pick, spread, xc, wg, wu, ab, count, wg_sem, wu_sem, a_sem):
+DB = 512
+ND = HID // DB
+
+
+def experts_kernel(xm_ref, gain_ref, router_ref, ids_ref, wg_hbm, wu_hbm, wd_hbm, y_ref,
+                   u, pick, spread, xc, ac, gc, wg, wu, wd, count, wg_sem, wu_sem, wd_sem):
     ring = wg.shape[0]
+    dring = wd.shape[0]
     steps = 2 * NF
+    dsteps = 2 * ND
     first_id = lax.axis_index("tp") * 2
 
     def in_copies(t):
@@ -393,9 +428,9 @@
         return (pltpu.make_async_copy(wg_hbm.at[t // NF, :, f], wg.at[s], wg_sem.at[s]),
                 pltpu.make_async_copy(wu_hbm.at[t // NF, :, f], wu.at[s], wu_sem.at[s]))
 
-    def out_copy(t):
-        f = pl.ds(pl.multiple_of((t % NF) * FB, FB), FB)
-        return pltpu.make_async_copy(ab.at[t % 2], a_hbm.at[t // NF, :, f], a_sem.at[t % 2])
+    def down_copy(t):
+        c = pl.ds(pl.multiple_of((t // 2) * DB, DB), DB)
+        return pltpu.make_async_copy(wd_hbm.at[t % 2, :, c], wd.at[t % dring], wd_sem.at[t % dring])
 
     for t in range(ring):
         for c in in_copies(t):
@@ -415,142 +450,124 @@
     g0, g1 = pair_gates(logits, id0, id1)
     lane = lax.broadcasted_iota(jnp.int32, (TOK, 128), 1)
     mine = (lane + first_id).astype(F32)
-    gates_ref[...] = jnp.where(mine == id0, g0, jnp.where(mine == id1, g1, 0.0))
-
-    def expert_rows(e):
+    gates = jnp.where(mine == id0, g0, jnp.where(mine == id1, g1, 0.0)).T
+
+    row = lax.broadcasted_iota(jnp.int32, (TOK, TOK), 0)
+    before = (row < lax.broadcasted_iota(jnp.int32, (TOK, TOK), 1)).astype(F32).astype(BF)
+    for e in range(2):
         target = first_id + e
         hit = ((ids_ref[0:1, :] == target) | (ids_ref[1:2, :] == target)).astype(F32)
-        before = lax.broadcasted_iota(jnp.int32, (TOK, TOK), 0) < lax.broadcasted_iota(jnp.int32, (TOK, TOK), 1)
-        hit8 = jnp.broadcast_to(hit, (8, TOK))
-        rank = dot(hit8.astype(BF), before.astype(F32).astype(BF))[0:1, :]
+        rank = dot(jnp.broadcast_to(hit, (8, TOK)).astype(BF), before)[0:1, :]
         place = jnp.where(hit > 0.5, rank, -1.0)
-        row = lax.broadcasted_iota(jnp.int32, (TOK, TOK), 0).astype(F32)
-        sel = (row == place).astype(F32)
+        sel = (row.astype(F32) == place).astype(F32)
         pick[...] = sel.astype(BF)
-        spread[...] = sel.T.astype(BF)
-        xc[...] = dot(pick[...], u[...]).astype(BF)
-        count[0] = (jnp.sum(hit).astype(jnp.int32) + 127) // 128
-
-    def block_step(t, _):
-        @pl.when(t % NF == 0)
-        def _():
-            expert_rows(t // NF)
-        s = t % ring
-        for c in in_copies(t):
-            c.wait()
-
-        @pl.when(t >= 2)
-        def _():
-            out_copy(t - 2).wait()
-        blocks = count[0]
-
-        def run(m):
-            g = dot(xc[0:m, :], wg[s])
-            up = dot(xc[0:m, :], wu[s])
-            act = (jax.nn.silu(g) * up).astype(BF)
-            ab[t % 2] = dot(spread[:, 0:m], act).astype(BF)
-
+        spread[e] = sel.T.astype(BF)
+        gc[e] = jnp.broadcast_to(jnp.sum(sel * gates[e:e + 1, :], axis=1, keepdims=True), (TOK, 128))
+        xc[e] = dot(pick[...], u[...]).astype(BF)
+        count[e] = (jnp.sum(hit).astype(jnp.int32) + 127) // 128
+
+    def by_blocks(blocks, run):
         for n in range(1, 5):
             @pl.when((blocks == n) if n > 1 else (blocks <= 1))
             def _(n=n):
                 run(128 * n)
-        out_copy(t).start()
+
+    def block_step(t, _):
+        e = t // NF
+        s = t % ring
+        f = pl.ds(pl.multiple_of((t % NF) * FB, FB), FB)
+        for c in in_copies(t):
+            c.wait()
+
+        def run(m):
+            g = dot(xc[e, 0:m, :], wg[s])
+            up = dot(xc[e, 0:m, :], wu[s])
+            ac[e, 0:m, f] = (jax.nn.silu(g) * up).astype(BF)
+
+        by_blocks(count[e], run)
 
         @pl.when(t + ring < steps)
         def _():
             for c in in_copies(t + ring):
                 c.start()
+
+        @pl.when((t + ring >= steps) & (t + ring < steps + dring))
+        def _():
+            down_copy(t + ring - steps).start()
         return 0
 
     lax.fori_loop(0, steps, block_step, 0)
-    for t in range(steps - 2, steps):
-        out_copy(t).wait()
-
-
-def gate_up_call(xm, gain, router_t, ids, wg, wu):
+
+    def down_step(t, _):
+        e = t % 2
+        s = t % dring
+        c = pl.ds(pl.multiple_of((t // 2) * DB, DB), DB)
+        down_copy(t).wait()
+
+        def run(m):
+            d = dot(ac[e, 0:m, :], wd[s])
+            gate = gc[e, 0:m, :]
+            parts = [(d[:, n * 128:(n + 1) * 128] * gate).astype(BF) for n in range(DB // 128)]
+            back = dot(spread[e, :, 0:m], jnp.concatenate(parts, axis=1))
+            y_ref[:, c] = (jnp.where(e == 0, 0.0, y_ref[:, c].astype(F32)) + back).astype(BF)
+
+        by_blocks(count[e], run)
+
+        @pl.when(t + dring < dsteps)
+        def _():
+            down_copy(t + dring).start()
+        return 0
+
+    lax.fori_loop(0, dsteps, down_step, 0)
+
+
+def experts_call(xm, gain, router_t, ids, wg, wu, wd):
     ring = 4
+    dring = 3
     return pl.pallas_call(
-        gate_up_kernel,
-        out_shape=(jax.ShapeDtypeStruct((2, TOK, FFN), BF), jax.ShapeDtypeStruct((TOK, 128), F32)),
-        in_specs=[vspec(), vspec(), vspec(), vspec(), hspec(), hspec()],
-        out_specs=(hspec(), vspec()),
+        experts_kernel,
+        out_shape=jax.ShapeDtypeStruct((TOK, HID), BF),
+        in_specs=[vspec(), vspec(), vspec(), vspec(), hspec(), hspec(), hspec()],
+        out_specs=vspec(),
         scratch_shapes=[
-            pltpu.VMEM((TOK, HID), BF), pltpu.VMEM((TOK, TOK), BF), pltpu.VMEM((TOK, TOK), BF), pltpu.VMEM((TOK, HID), BF),
-            pltpu.VMEM((ring, HID, FB), BF), pltpu.VMEM((ring, HID, FB), BF), pltpu.VMEM((2, TOK, FB), BF),
-            pltpu.SMEM((1,), jnp.int32),
-            pltpu.SemaphoreType.DMA((ring,)), pltpu.SemaphoreType.DMA((ring,)), pltpu.SemaphoreType.DMA((2,)),
+            pltpu.VMEM((TOK, HID), BF), pltpu.VMEM((TOK, TOK), BF), pltpu.VMEM((2, TOK, TOK), BF), pltpu.VMEM((2, TOK, HID), BF),
+            pltpu.VMEM((2, TOK, FFN), BF), pltpu.VMEM((2, TOK, 128), F32),
+            pltpu.VMEM((ring, HID, FB), BF), pltpu.VMEM((ring, HID, FB), BF), pltpu.VMEM((dring, FFN, DB), BF),
+            pltpu.SMEM((2,), jnp.int32),
+            pltpu.SemaphoreType.DMA((ring,)), pltpu.SemaphoreType.DMA((ring,)), pltpu.SemaphoreType.DMA((dring,)),
         ],
         compiler_params=pltpu.CompilerParams(vmem_limit_bytes=VMEM_BYTES),
-        name="gate_up",
-    )(xm, gain, router_t, ids, wg, wu)
-
-
-def down_kernel(xm_ref, a_hbm, gates_ref, wd_hbm, out_ref, a, wd, acc, a_sem, wd_sem, part, r1, cs, r2, fin, r3, sems):
-    chunks, width = part.shape[0], part.shape[2]
-    ring = wd.shape[0]
-    total = 2 * chunks
-
-    def wd_copy(t):
-        cols = pl.ds(pl.multiple_of((t // 2) * width, width), width)
-        return pltpu.make_async_copy(wd_hbm.at[t % 2, :, cols], wd.at[t % ring], wd_sem.at[t % ring])
-
-    for e in range(2):
-        pltpu.make_async_copy(a_hbm.at[e], a.at[e], a_sem.at[e]).start()
-        wd_copy(e).start()
-    for t in range(2, ring):
-        wd_copy(t).start()
-    net = PairSum(part, r1, cs, r2, fin, r3, sems)
+        name="experts",
+    )(xm, gain, router_t, ids, wg, wu, wd)
+
+
+def sum_kernel(xm_ref, y_ref, out_ref, r1, cs, r2, fin, r3, sems):
+    chunks, width = r1.shape[0], r1.shape[2]
+    net = PairSum(lambda j, rows: y_ref.at[rows, pl.ds(pl.multiple_of(j * width, width), width)], r1, cs, r2, fin, r3, sems)
     net.greet()
-    for e in range(2):
-        pltpu.make_async_copy(a_hbm.at[e], a.at[e], a_sem.at[e]).wait()
-
-    def chunk_step(j, _):
-        for e in range(2):
-            t = 2 * j + e
-            wd_copy(t).wait()
-            prod = dot(a[e], wd[t % ring]) * gates_ref[:, e:e + 1]
-            if e == 0:
-                acc[...] = prod
-            else:
-                part[j] = (acc[...] + prod).astype(BF)
-
-            @pl.when(t + ring < total)
-            def _():
-                wd_copy(t + ring).start()
+    for j in range(chunks):
         net.first(j)
 
-        @pl.when(j >= 1)
-        def _():
-            net.second(j - 1)
-        return 0
-
-    lax.fori_loop(0, chunks, chunk_step, 0)
-    net.second(chunks - 1)
-    for j in range(chunks):
-        net.third(j, xm_ref, slice(j * width, (j + 1) * width))
-        if j >= 1:
-            net.last(j - 1, out_ref, slice((j - 1) * width, j * width))
-    net.last(chunks - 1, out_ref, slice((chunks - 1) * width, chunks * width))
-
-
-def down_call(xm, a, gates, wd):
-    chunks = 4
+    def step(j, _):
+        net.second(j)
+        return 0
+
+    lax.fori_loop(0, chunks, step, 0)
+    net.finish(chunks, xm_ref, out_ref)
+
+
+def sum_call(xm, y):
+    chunks = 8
     width = HID // chunks
-    ring = 3
     return pl.pallas_call(
-        down_kernel,
+        sum_kernel,
         out_shape=jax.ShapeDtypeStruct((TOK, HID), BF),
-        in_specs=[vspec(), hspec(), vspec(), hspec()],
+        in_specs=[vspec(), vspec()],
         out_specs=vspec(),
-        scratch_shapes=[
-            pltpu.VMEM((2, TOK, FFN), BF),
-            pltpu.VMEM((ring, FFN, width), BF),
-            pltpu.VMEM((TOK, width), F32),
-            pltpu.SemaphoreType.DMA((2,)), pltpu.SemaphoreType.DMA((ring,)),
-        ] + pair_scratch(chunks, width),
-        compiler_params=pltpu.CompilerParams(vmem_limit_bytes=VMEM_BYTES, collective_id=1, has_side_effects=True),
-        name="down_sum",
-    )(xm, a, gates, wd)
+        scratch_shapes=pair_scratch(chunks, width),
+        compiler_params=pltpu.CompilerParams(vmem_limit_bytes=32 * 1024 * 1024, collective_id=1, has_side_effects=True),
+        name="expert_sum",
+    )(xm, y)
 
 
 def rope_tables():
@@ -566,14 +583,13 @@
 
     def local_step(x, k_cache, v_cache, positions, att_ids, mlp_ids, norm_att, w_kv, router_att, w_query, w_out, norm_mlp, router_mlp, w_gate, w_up, w_down):
         flat = (TOK * SLOTS * HEADS, HD)
-        wkv = w_kv.reshape(HID, HEADS, 2, HD).transpose(0, 2, 1, 3).reshape(HID, 2 * HEADS * HD)
-        rows = jnp.concatenate([att_ids.T, positions[None, :]], axis=0)
+        wkv = w_kv.reshape(HID, HEADS, 2, HD).transpose(0, 2, 1, 3).reshape(HID * 2 * HEADS, HD)
         k_out, v_out, o, meta = attention_call(
-            x, norm_att[None, :], wkv, router_att.T, w_query, k_cache.reshape(flat), v_cache.reshape(flat), rows,
+            x, norm_att[None, :], wkv, router_att.T, w_query, k_cache.reshape(flat), v_cache.reshape(flat), att_ids.T, positions[None, :],
             jnp.asarray(cos_tab), jnp.asarray(sin_tab))
         xm = project_call(x, o, meta, w_out)
-        a, gates = gate_up_call(xm, norm_mlp[None, :], router_mlp.T, mlp_ids.T, w_gate, w_up)
-        x_out = down_call(xm, a, gates, w_down)
+        y = experts_call(xm, norm_mlp[None, :], router_mlp.T, mlp_ids.T, w_gate, w_up, w_down)
+        x_out = sum_call(xm, y)
         return x_out, k_out.reshape(k_cache.shape), v_out.reshape(v_cache.shape)
 
     token_spec = P('dp', None)

time: 183 us -> 166 us (0.907)
  Pallas kernels: 169 us -> 161 us
  local copies, waits for them, and re-layouts: 10.8 us -> 4.5 us
    pallas_call x2, Pallas kernels: 95.3 us -> 85 us  [the longest x1 46.4 us: experts_call(): pl.pallas_call(experts_kernel, out_shape=jax.ShapeDtypeStruct((TOK, HID),...]
    reshape x1 -> x0, local copies, waits for them, and re-layouts: 7.69 us -> none  [local_step(): w_kv.reshape(HID, HEADS, 2, HD).transpose(0, 2, 1, 3)]
    pallas_call x1, Pallas kernels: 33.7 us -> 35.9 us  [attention_call(): pl.pallas_call(attention_kernel, out_shape=(cache, cache, jax.ShapeDtypeS...]
    unnamed x1 -> x5, local copies, waits for them, and re-layouts: 3.16 us -> 4.5 us
where the time goes in v2:
time: 166 us
  Pallas kernels  161 us (97%)
  local copies, waits for them, and re-layouts  4.5 us (3%)
    pallas_call x1, Pallas kernels, experts_call(): pl.pallas_call(experts_kernel, out_shape=jax.ShapeDtypeStruct((TOK, HID),...  46.4 us
    pallas_call x1, Pallas kernels, project_call(): pl.pallas_call(project_kernel, out_shape=jax.ShapeDtypeStruct((TOK, HID),...  39.8 us
    pallas_call x1, Pallas kernels, sum_call(): pl.pallas_call(sum_kernel, out_shape=jax.ShapeDtypeStruct((TOK, HID), BF)...  38.7 us
    pallas_call x1, Pallas kernels, attention_call(): pl.pallas_call(attention_kernel, out_shape=(cache, cache, jax.ShapeDtypeS...  35.9 us
    unnamed x5, local copies, waits for them, and re-layouts  4.5 us

profile of v2, /device:TPU:0, one launch (start us, length us, event | category | flops | bytes accessed | tf_op | source)
XLA Modules:
  0.0 166.0 jit_solution(16267638215886342267)
XLA Ops:
  0.6 35.9 %attention.1 = (bf16[32768,128]{1,0:T(8,128)(2,1)}, bf16[32768,128]{1,0:T(8,128)(2,1)}, bf16[512,1024]{1,0:T(8,128)(2,1)}, f32[512,128]{1,0:T(8,128)}) custom-call(bf16[512,2048]{1,0:T(8,128)(2,1)} %x_hbm.1, f32[1,2048]{1,0:T(1,128)} %bitcast.21, bf16[16384,128]{1,0:T(8,128)(2,1)} %bitcast.18, bf16[8,2048]{1,0:T(8,128)(2,1)} %bitcast.19, ...), custom_call_target="tpu_custom_call" | custom-call | tf_op jit(solution)/shard_map/attention/pallas_call | solution.py:235
  36.6 39.8 %project_sum.1.xm_ref = bf16[512,2048]{1,0:T(8,128)(2,1)} custom-call(bf16[512,2048]{1,0:T(8,128)(2,1)} %x_hbm.1, bf16[512,1024]{1,0:T(8,128)(2,1)} %get-tuple-element.7.o_ref, f32[512,128]{1,0:T(8,128)} %get-tuple-element.8.meta_ref, bf16[8,512,2048]{2,1,0:T(8,128)(2,1)} %wo_hbm.1), custom_call_target="tpu_custom_call" | custom-call | tf_op jit(solution)/shard_map/project_sum/pallas_call | solution.py:392
  76.4 46.4 %experts.1.y_ref = bf16[512,2048]{1,0:T(8,128)(2,1)} custom-call(bf16[512,2048]{1,0:T(8,128)(2,1)} %project_sum.1.xm_ref, f32[1,2048]{1,0:T(1,128)} %bitcast.22, bf16[8,2048]{1,0:T(8,128)(2,1)} %bitcast.20, s32[2,512]{1,0:T(2,128)} %bitcast.24, bf16[2,2048,5632]{2,1,0:T(8,128)(2,1)} %wg_hbm.1, bf16[2,2048,5632]{2,1,0:T(8,128)(2,1)} %wu_hbm.1, ...), custom_call_target="tpu_custom_call" | custom-call | tf_op jit(solution)/shard_map/experts/pallas_call | solution.py:527
  122.8 0.0 copy-start
  122.8 1.6 copy-done
  124.4 0.0 copy-start.1
  124.4 1.6 copy-done.1
  126.0 38.7 %expert_sum.1 = bf16[512,2048]{1,0:T(8,128)(2,1)S(1)} custom-call(bf16[512,2048]{1,0:T(8,128)(2,1)S(1)} %copy-done, bf16[512,2048]{1,0:T(8,128)(2,1)S(1)} %copy-done.1), custom_call_target="tpu_custom_call" | custom-call | tf_op jit(solution)/shard_map/expert_sum/pallas_call | solution.py:562
  164.7 1.3 copy.23
Async XLA Ops:
  122.8 1.6 copy-start
  124.4 1.6 copy-start.1

commit v3 on v2

--- a/solution.py
+++ b/solution.py
@@ -69,6 +69,8 @@
                      wkv_sem, wq_sem, kin_sem, vin_sem, ko_sem, vo_sem):
     ring = wq.shape[0]
     steps = TOK // SUB
+    depth = kin.shape[0]
+    back = kout.shape[0]
     cache_rows = SUB * SLOTS * HEADS
 
     def cache_rows_at(i):
@@ -78,20 +80,21 @@
         return pltpu.make_async_copy(wq_hbm.at[e], wq.at[e % ring], wq_sem.at[e % ring])
 
     def in_copies(i):
-        s = i % 2
+        s = i % depth
         return (pltpu.make_async_copy(kc_hbm.at[cache_rows_at(i)], kin.at[s], kin_sem.at[s]),
                 pltpu.make_async_copy(vc_hbm.at[cache_rows_at(i)], vin.at[s], vin_sem.at[s]))
 
     def out_copies(i):
-        s = i % 2
+        s = i % back
         return (pltpu.make_async_copy(kout.at[s], ko_hbm.at[cache_rows_at(i)], ko_sem.at[s]),
                 pltpu.make_async_copy(vout.at[s], vo_hbm.at[cache_rows_at(i)], vo_sem.at[s]))
 
     wkv_copy = pltpu.make_async_copy(wkv_hbm, wkv_raw, wkv_sem)
+    wq_copy(0).start()
     wkv_copy.start()
-    for e in range(ring):
+    for e in range(1, ring):
         wq_copy(e).start()
-    for i in range(2):
+    for i in range(depth):
         for c in in_copies(i):
             c.start()
 
@@ -125,19 +128,7 @@
 
     wkv_copy.wait()
     half = HEADS * HD
-    deep = wkv_wide.shape[0] // 8
-
-    def relayout_step(i, _):
-        wkv_wide[...] = wkv_raw[pl.ds(pl.multiple_of(i * deep * 8, deep * 8), deep * 8), :].astype(F32)
-        for j in range(8):
-            wkv[pl.ds(pl.multiple_of(i * deep, deep), deep), j * HD:(j + 1) * HD] = wkv_wide[pl.ds(j, deep, stride=8), :].astype(BF)
-        return 0
-
-    lax.fori_loop(0, HID // deep, relayout_step, 0)
-    kf = dot(h[...], wkv[:, 0:half])
-    for n in range(HEADS):
-        kvb[:, n * HD:(n + 1) * HD] = rope(kf[:, n * HD:(n + 1) * HD]).astype(BF)
-    kvb[:, half:2 * half] = dot(h[...], wkv[:, half:2 * half]).astype(BF)
+    deep = HID // ATT_E
 
     def query_step(e, _):
         wq_copy(e).wait()
@@ -147,6 +138,9 @@
         m1 = meta_ref[:, 1:2] == ef
         qf[:, 0:half] = jnp.where(m0, qe, qf[:, 0:half])
         qf[:, half:2 * half] = jnp.where(m1, qe, qf[:, half:2 * half])
+        wkv_wide[...] = wkv_raw[pl.ds(pl.multiple_of(e * deep * 8, deep * 8), deep * 8), :].astype(F32)
+        for j in range(8):
+            wkv[pl.ds(pl.multiple_of(e * deep, deep), deep), j * HD:(j + 1) * HD] = wkv_wide[pl.ds(j, deep, stride=8), :].astype(BF)
 
         @pl.when(e + ring < ATT_E)
         def _():
@@ -154,6 +148,10 @@
         return 0
 
     lax.fori_loop(0, ATT_E, query_step, 0)
+    kf = dot(h[...], wkv[:, 0:half])
+    for n in range(HEADS):
+        kvb[:, n * HD:(n + 1) * HD] = rope(kf[:, n * HD:(n + 1) * HD]).astype(BF)
+    kvb[:, half:2 * half] = dot(h[...], wkv[:, half:2 * half]).astype(BF)
     for n in range(2 * HEADS):
         c = slice(n * HD, (n + 1) * HD)
         qb[:, c] = rope(qf[:, c]).astype(BF)
@@ -169,7 +167,8 @@
     upper = row32 < rows // 2
 
     def cache_step(i, _):
-        s = i % 2
+        s = i % depth
+        so = i % back
         r = pl.ds(pl.multiple_of(i * SUB, SUB), SUB)
         for j in range(2 * HEADS):
             q8[pl.ds(j, SUB, stride=8), :] = qb[r, j * HD:(j + 1) * HD].astype(F32)
@@ -178,58 +177,72 @@
             vn8[pl.ds(j, SUB, stride=8), :] = kvb[r, half + n * HD:half + (n + 1) * HD].astype(F32)
             pos8[pl.ds(j, SUB, stride=8), :] = jnp.broadcast_to(meta_ref[r, 4:5], (SUB, 128))
 
-        @pl.when(i >= 2)
-        def _():
-            for c in out_copies(i - 2):
+        @pl.when(i >= back)
+        def _():
+            for c in out_copies(i - back):
                 c.wait()
         for c in in_copies(i):
             c.wait()
 
+        def group_rows(g):
+            return slice(g * group * 64, (g + 1) * group * 64), slice(g * group * 8, (g + 1) * group * 8)
+
         for part in range(SUB // 32):
+            groups = range(part * 8, part * 8 + 8, 2)
             scores = []
-            for g in range(8):
-                b0 = part * 32 + g * group
-                rr = slice(b0 * 64, (b0 + group) * 64)
-                r8 = slice(b0 * 8, (b0 + group) * 8)
-                hit = slot_id[None] == pos8[r8, :].reshape(group, 1, 8, 128)
-                old_k = kin[s, rr, :].astype(F32).reshape(group, 8, 8, 128)
-                new_k = jnp.where(hit, kn8[r8, :].reshape(group, 1, 8, 128), old_k).astype(BF).reshape(group * 64, 128)
-                kout[s, rr, :] = new_k
-                old_v = vin[s, rr, :].astype(F32).reshape(group, 8, 8, 128)
-                new_v = jnp.where(hit, vn8[r8, :].reshape(group, 1, 8, 128), old_v).astype(BF).reshape(group * 64, 128)
-                vout[s, rr, :] = new_v
-                sc = dot_nt(q8[r8, :].astype(BF), new_k)
-                scores.append(jnp.concatenate([sc[0:rows // 2, 0:128], sc[rows // 2:, 128:256]], axis=0))
-            for g in range(8):
-                b0 = part * 32 + g * group
-                rr = slice(b0 * 64, (b0 + group) * 64)
-                r8 = slice(b0 * 8, (b0 + group) * 8)
-                valid = own_part & (slot32 <= pos8[r8, :])
-                sc = jnp.where(valid, scores[g] * scale, -1e30)
-                ex = jnp.exp(sc - jnp.max(sc, axis=1, keepdims=True))
-                w = ex / jnp.sum(ex, axis=1, keepdims=True)
-                wide = jnp.concatenate([jnp.where(upper, w, 0.0), jnp.where(upper, 0.0, w)], axis=1).astype(BF)
-                o8[r8, :] = dot(wide, vout[s, rr, :])
+            for g0 in groups:
+                keys, queries = [], []
+                for g in (g0, g0 + 1):
+                    rr, r8 = group_rows(g)
+                    hit = slot_id[None] == pos8[r8, :].reshape(group, 1, 8, 128)
+                    old_k = kin[s, rr, :].astype(F32).reshape(group, 8, 8, 128)
+                    new_k = jnp.where(hit, kn8[r8, :].reshape(group, 1, 8, 128), old_k).reshape(group * 64, 128).astype(BF)
+                    kout[so, rr, :] = new_k
+                    old_v = vin[s, rr, :].astype(F32).reshape(group, 8, 8, 128)
+                    new_v = jnp.where(hit, vn8[r8, :].reshape(group, 1, 8, 128), old_v).reshape(group * 64, 128).astype(BF)
+                    vout[so, rr, :] = new_v
+                    keys.append(new_k)
+                    queries.append(q8[r8, :].astype(BF))
+                none = jnp.zeros((rows, 128), BF)
+                both = jnp.concatenate([jnp.concatenate([queries[0], none], axis=1), jnp.concatenate([none, queries[1]], axis=1)], axis=0)
+                sc = dot_nt(both, jnp.concatenate(keys, axis=1))
+                for b in (0, rows):
+                    scores.append(jnp.concatenate([sc[b:b + rows // 2, 0:128], sc[b + rows // 2:b + rows, 128:256]], axis=0))
+            for n, g0 in enumerate(groups):
+                wides, values = [], []
+                for b in range(2):
+                    rr, r8 = group_rows(g0 + b)
+                    valid = own_part & (slot32 <= pos8[r8, :])
+                    sc = jnp.where(valid, scores[2 * n + b] * scale, -1e30)
+                    ex = jnp.exp(sc - jnp.max(sc, axis=1, keepdims=True))
+                    w = ex / jnp.sum(ex, axis=1, keepdims=True)
+                    wides.append(jnp.concatenate([jnp.where(upper, w, 0.0), jnp.where(upper, 0.0, w)], axis=1).astype(BF))
+                    values.append(vout[so, rr, :])
+                res = dot(jnp.concatenate(wides, axis=0), jnp.concatenate(values, axis=1))
+                for b in range(2):
+                    o8[group_rows(g0 + b)[1], :] = res[b * rows:(b + 1) * rows, b * 128:(b + 1) * 128]
 
         for c in out_copies(i):
             c.start()
 
-        @pl.when(i + 2 < steps)
-        def _():
-            for c in in_copies(i + 2):
+        @pl.when(i + depth < steps)
+        def _():
+            for c in in_copies(i + depth):
                 c.start()
         for j in range(2 * HEADS):
             o_ref[r, j * HD:(j + 1) * HD] = o8[pl.ds(j, SUB, stride=8), :].astype(BF)
         return 0
 
     lax.fori_loop(0, steps, cache_step, 0)
-    for i in range(steps - 2, steps):
+    for i in range(steps - back, steps):
         for c in out_copies(i):
             c.wait()
 
 
 def attention_call(x, gain, wkv, router_t, wq, kc, vc, ids, pos, cos_tab, sin_tab):
     ring = 4
+    depth = 2
+    back = 2
     cache_rows = SUB * SLOTS * HEADS
     cache = jax.ShapeDtypeStruct(kc.shape, BF)
     return pl.pallas_call(
@@ -247,11 +260,11 @@
             pltpu.VMEM((TOK, 2 * HEADS * HD), BF),
             pltpu.VMEM((SUB * 8, 128), F32), pltpu.VMEM((SUB * 8, 128), F32), pltpu.VMEM((SUB * 8, 128), F32),
             pltpu.VMEM((SUB * 8, 128), F32), pltpu.VMEM((SUB * 8, 128), F32),
-            pltpu.VMEM((2, cache_rows, HD), BF), pltpu.VMEM((2, cache_rows, HD), BF),
-            pltpu.VMEM((2, cache_rows, HD), BF), pltpu.VMEM((2, cache_rows, HD), BF),
+            pltpu.VMEM((depth, cache_rows, HD), BF), pltpu.VMEM((depth, cache_rows, HD), BF),
+            pltpu.VMEM((back, cache_rows, HD), BF), pltpu.VMEM((back, cache_rows, HD), BF),
             pltpu.SemaphoreType.DMA, pltpu.SemaphoreType.DMA((ring,)),
-            pltpu.SemaphoreType.DMA((2,)), pltpu.SemaphoreType.DMA((2,)),
-            pltpu.SemaphoreType.DMA((2,)), pltpu.SemaphoreType.DMA((2,)),
+            pltpu.SemaphoreType.DMA((depth,)), pltpu.SemaphoreType.DMA((depth,)),
+            pltpu.SemaphoreType.DMA((back,)), pltpu.SemaphoreType.DMA((back,)),
         ],
         compiler_params=pltpu.CompilerParams(vmem_limit_bytes=VMEM_BYTES),
         name="attention",
@@ -264,6 +277,7 @@
 class PairSum:
     def __init__(self, part_at, r1, cs, r2, fin, r3, sems):
         self.part_at, self.r1, self.cs, self.r2, self.fin, self.r3 = part_at, r1, cs, r2, fin, r3
+        self.own_at = lambda j: part_at(j, self.own)
         self.sems = sems
         self.width = r1.shape[2]
         me = lax.axis_index("tp")
@@ -294,7 +308,7 @@
 
     def second(self, j):
         self.copy(0, j).wait()
-        self.cs[j] = (self.part_at(j, self.own)[...].astype(F32) + self.r1[j].astype(F32)).astype(BF)
+        self.cs[j] = (self.own_at(j)[...].astype(F32) + self.r1[j].astype(F32)).astype(BF)
         self.copy(1, j).start()
 
     def third(self, j, base_ref):
@@ -339,7 +353,8 @@
     x_copy.start()
     net = PairSum(lambda j, rows: part.at[j, rows], r1, cs, r2, fin, r3, sems)
     net.greet()
-    for e in range(ATT_E):
+
+    def prepare(e):
         m0 = meta_ref[:, 0:1] == float(e)
         m1 = meta_ref[:, 1:2] == float(e)
         f0 = jnp.broadcast_to(jnp.where(m0, 1.0, 0.0), (TOK, 128)).astype(BF)
@@ -350,36 +365,40 @@
         gate = jnp.where(m0, meta_ref[:, 2:3], jnp.where(m1, meta_ref[:, 3:4], 0.0))
         gb[e] = jnp.broadcast_to(gate, (TOK, 128))
 
-    def chunk_step(j, _):
+    def project(j, fresh):
         wo_copy(j).wait()
         slot = j % ring
-
-        def expert_step(e, _):
+        for e in range(ATT_E):
+            if fresh:
+                prepare(e)
             prod = dot(oe[e], wo[slot, e])
-            gate = gb[e]
             for n in range(width // 128):
                 c = slice(n * 128, (n + 1) * 128)
-                acc[:, c] = jnp.where(e == 0, 0.0, acc[:, c]) + gate * prod[:, c]
-            return 0
-
-        lax.fori_loop(0, ATT_E, expert_step, 0)
-        part[j] = acc[...].astype(BF)
+                term = gb[e] * prod[:, c]
+                if e == 0:
+                    acc[:, c] = term
+                elif e < ATT_E - 1:
+                    acc[:, c] += term
+                else:
+                    part[j, :, c] = (acc[:, c] + term).astype(BF)
+        net.first(j)
+
+    def chunk_step(j, _):
+        project(j, False)
 
         @pl.when(j + ring < chunks)
         def _():
             wo_copy(j + ring).start()
-        net.first(j)
-
-        @pl.when(j == 0)
-        def _():
-            net.second(j)
 
         @pl.when(j >= 2)
         def _():
             net.second(j - 1)
         return 0
 
-    lax.fori_loop(0, chunks, chunk_step, 0)
+    project(0, True)
+    wo_copy(ring).start()
+    net.second(0)
+    lax.fori_loop(1, chunks, chunk_step, 0)
     net.second(chunks - 1)
     x_copy.wait()
     net.finish(chunks, xv, xm_ref)
@@ -412,6 +431,7 @@
 NF = FFN // FB
 DB = 512
 ND = HID // DB
+ROW_STEPS = (128, 192, 256, 320, 384, 512)
 
 
 def experts_kernel(xm_ref, gain_ref, router_ref, ids_ref, wg_hbm, wu_hbm, wd_hbm, y_ref,
@@ -423,10 +443,10 @@
     first_id = lax.axis_index("tp") * 2
 
     def in_copies(t):
-        f = pl.ds(pl.multiple_of((t % NF) * FB, FB), FB)
+        f = pl.ds(pl.multiple_of((t // 2) * FB, FB), FB)
         s = t % ring
-        return (pltpu.make_async_copy(wg_hbm.at[t // NF, :, f], wg.at[s], wg_sem.at[s]),
-                pltpu.make_async_copy(wu_hbm.at[t // NF, :, f], wu.at[s], wu_sem.at[s]))
+        return (pltpu.make_async_copy(wg_hbm.at[t % 2, :, f], wg.at[s], wg_sem.at[s]),
+                pltpu.make_async_copy(wu_hbm.at[t % 2, :, f], wu.at[s], wu_sem.at[s]))
 
     def down_copy(t):
         c = pl.ds(pl.multiple_of((t // 2) * DB, DB), DB)
@@ -464,18 +484,18 @@
         spread[e] = sel.T.astype(BF)
         gc[e] = jnp.broadcast_to(jnp.sum(sel * gates[e:e + 1, :], axis=1, keepdims=True), (TOK, 128))
         xc[e] = dot(pick[...], u[...]).astype(BF)
-        count[e] = (jnp.sum(hit).astype(jnp.int32) + 127) // 128
+        count[e] = (jnp.sum(hit).astype(jnp.int32) + 63) // 64
 
     def by_blocks(blocks, run):
-        for n in range(1, 5):
-            @pl.when((blocks == n) if n > 1 else (blocks <= 1))
-            def _(n=n):
-                run(128 * n)
+        for low, high in zip((0,) + ROW_STEPS[:-1], ROW_STEPS):
+            @pl.when((blocks * 64 > low) & (blocks * 64 <= high) if low else blocks * 64 <= high)
+            def _(high=high):
+                run(high)
 
     def block_step(t, _):
-        e = t // NF
+        e = t % 2
         s = t % ring
-        f = pl.ds(pl.multiple_of((t % NF) * FB, FB), FB)
+        f = pl.ds(pl.multiple_of((t // 2) * FB, FB), FB)
         for c in in_copies(t):
             c.wait()
 
@@ -541,19 +561,30 @@
     )(xm, gain, router_t, ids, wg, wu, wd)
 
 
-def sum_kernel(xm_ref, y_ref, out_ref, r1, cs, r2, fin, r3, sems):
+def sum_kernel(xm_hbm, y_hbm, out_ref, xv, yv, in_sem, r1, cs, r2, fin, r3, sems):
     chunks, width = r1.shape[0], r1.shape[2]
-    net = PairSum(lambda j, rows: y_ref.at[rows, pl.ds(pl.multiple_of(j * width, width), width)], r1, cs, r2, fin, r3, sems)
+
+    def y_at(j, rows):
+        return y_hbm.at[rows, pl.ds(pl.multiple_of(j * width, width), width)]
+
+    net = PairSum(y_at, r1, cs, r2, fin, r3, sems)
+    x_copy = pltpu.make_async_copy(xm_hbm.at[net.own], xv.at[net.own], in_sem.at[0])
+    y_copy = pltpu.make_async_copy(y_hbm.at[net.own], yv.at[net.own], in_sem.at[1])
+    y_copy.start()
+    x_copy.start()
     net.greet()
     for j in range(chunks):
         net.first(j)
+    y_copy.wait()
+    net.own_at = lambda j: yv.at[net.own, net.cols(j)]
 
     def step(j, _):
         net.second(j)
         return 0
 
     lax.fori_loop(0, chunks, step, 0)
-    net.finish(chunks, xm_ref, out_ref)
+    x_copy.wait()
+    net.finish(chunks, xv, out_ref)
 
 
 def sum_call(xm, y):
@@ -562,10 +593,10 @@
     return pl.pallas_call(
         sum_kernel,
         out_shape=jax.ShapeDtypeStruct((TOK, HID), BF),
-        in_specs=[vspec(), vspec()],
+        in_specs=[hspec(), hspec()],
         out_specs=vspec(),
-        scratch_shapes=pair_scratch(chunks, width),
-        compiler_params=pltpu.CompilerParams(vmem_limit_bytes=32 * 1024 * 1024, collective_id=1, has_side_effects=True),
+        scratch_shapes=[pltpu.VMEM((TOK, HID), BF), pltpu.VMEM((TOK, HID), BF), pltpu.SemaphoreType.DMA((2,))] + pair_scratch(chunks, width),
+        compiler_params=pltpu.CompilerParams(vmem_limit_bytes=61 * 1024 * 1024, collective_id=1, has_side_effects=True),
         name="expert_sum",
     )(xm, y)
 

time: 166 us -> 158 us (0.952)
  Pallas kernels: 161 us -> 155 us
    pallas_call x1, Pallas kernels: 38.7 us -> 36.1 us  [sum_call(): pl.pallas_call(sum_kernel, out_shape=jax.ShapeDtypeStruct((TOK, HID), BF)...]
    pallas_call x1, Pallas kernels: 39.8 us -> 37.4 us  [project_call(): pl.pallas_call(project_kernel, out_shape=jax.ShapeDtypeStruct((TOK, HID),...]
    unnamed x5 -> x1, local copies, waits for them, and re-layouts: 4.5 us -> 3.16 us
where the time goes in v3:
time: 158 us; the launch traced here: 159 us
  Pallas kernels  155 us (98%)
  local copies, waits for them, and re-layouts  3.16 us (2%)
    pallas_call x1, Pallas kernels, experts_call(): pl.pallas_call(experts_kernel, out_shape=jax.ShapeDtypeStruct((TOK, HID),...  46.4 us
    pallas_call x1, Pallas kernels, project_call(): pl.pallas_call(project_kernel, out_shape=jax.ShapeDtypeStruct((TOK, HID),...  37.4 us
    pallas_call x1, Pallas kernels, sum_call(): pl.pallas_call(sum_kernel, out_shape=jax.ShapeDtypeStruct((TOK, HID), BF)...  36.1 us
    pallas_call x1, Pallas kernels, attention_call(): pl.pallas_call(attention_kernel, out_shape=(cache, cache, jax.ShapeDtypeS...  35.4 us

profile of v3, /device:TPU:0, one launch (start us, length us, event | category | flops | bytes accessed | tf_op | source)
XLA Modules:
  0.0 159.0 jit_solution(15752640556316175392)
XLA Ops:
  0.6 35.4 %attention.1 = (bf16[32768,128]{1,0:T(8,128)(2,1)}, bf16[32768,128]{1,0:T(8,128)(2,1)}, bf16[512,1024]{1,0:T(8,128)(2,1)}, f32[512,128]{1,0:T(8,128)}) custom-call(bf16[512,2048]{1,0:T(8,128)(2,1)} %x_hbm.1, f32[1,2048]{1,0:T(1,128)} %bitcast.21, bf16[16384,128]{1,0:T(8,128)(2,1)} %bitcast.18, bf16[8,2048]{1,0:T(8,128)(2,1)} %bitcast.19, ...), custom_call_target="tpu_custom_call" | custom-call | tf_op jit(solution)/shard_map/attention/pallas_call | solution.py:248
  36.0 37.4 %project_sum.1.xm_ref.xm_hbm = bf16[512,2048]{1,0:T(8,128)(2,1)} custom-call(bf16[512,2048]{1,0:T(8,128)(2,1)} %x_hbm.1, bf16[512,1024]{1,0:T(8,128)(2,1)} %get-tuple-element.7.o_ref, f32[512,128]{1,0:T(8,128)} %get-tuple-element.8.meta_ref, bf16[8,512,2048]{2,1,0:T(8,128)(2,1)} %wo_hbm.1), custom_call_target="tpu_custom_call" | custom-call | tf_op jit(solution)/shard_map/project_sum/pallas_call | solution.py:411
  73.4 46.4 %experts.1.y_hbm = bf16[512,2048]{1,0:T(8,128)(2,1)} custom-call(bf16[512,2048]{1,0:T(8,128)(2,1)} %project_sum.1.xm_ref.xm_hbm, f32[1,2048]{1,0:T(1,128)} %bitcast.22, bf16[8,2048]{1,0:T(8,128)(2,1)} %bitcast.20, s32[2,512]{1,0:T(2,128)} %bitcast.24, bf16[2,2048,5632]{2,1,0:T(8,128)(2,1)} %wg_hbm.1, bf16[2,2048,5632]{2,1,0:T(8,128)(2,1)} %wu_hbm.1, ...), custom_call_target="tpu_custom_call" | custom-call | tf_op jit(solution)/shard_map/experts/pallas_call | solution.py:547
  119.8 36.1 %expert_sum.1 = bf16[512,2048]{1,0:T(8,128)(2,1)} custom-call(bf16[512,2048]{1,0:T(8,128)(2,1)} %project_sum.1.xm_ref.xm_hbm, bf16[512,2048]{1,0:T(8,128)(2,1)} %experts.1.y_hbm), custom_call_target="tpu_custom_call" | custom-call | tf_op jit(solution)/shard_map/expert_sum/pallas_call | solution.py:593
  155.9 3.2 %copy.23 = bf16[512,2048]{1,0:T(8,128)(2,1)} copy(bf16[512,2048]{1,0:T(8,128)(2,1)} %expert_sum.1) | data formatting | bytes 4194304

commit v4 on v3

--- a/solution.py
+++ b/solution.py
@@ -94,9 +94,6 @@
     wkv_copy.start()
     for e in range(1, ring):
         wq_copy(e).start()
-    for i in range(depth):
-        for c in in_copies(i):
-            c.start()
 
     gain = gain_ref[...]
 
@@ -132,6 +129,11 @@
 
     def query_step(e, _):
         wq_copy(e).wait()
+
+        @pl.when(e < depth)
+        def _():
+            for c in in_copies(e):
+                c.start()
         ef = e.astype(F32)
         qe = dot(h[...], wq[e % ring])
         m0 = meta_ref[:, 0:1] == ef
@@ -241,7 +243,7 @@
 
 def attention_call(x, gain, wkv, router_t, wq, kc, vc, ids, pos, cos_tab, sin_tab):
     ring = 4
-    depth = 2
+    depth = 4
     back = 2
     cache_rows = SUB * SLOTS * HEADS
     cache = jax.ShapeDtypeStruct(kc.shape, BF)
@@ -354,16 +356,17 @@
     net = PairSum(lambda j, rows: part.at[j, rows], r1, cs, r2, fin, r3, sems)
     net.greet()
 
+    id0, id1, g0, g1 = (jnp.broadcast_to(meta_ref[:, n:n + 1], (TOK, 128)) for n in range(4))
+
     def prepare(e):
-        m0 = meta_ref[:, 0:1] == float(e)
-        m1 = meta_ref[:, 1:2] == float(e)
-        f0 = jnp.broadcast_to(jnp.where(m0, 1.0, 0.0), (TOK, 128)).astype(BF)
-        f1 = jnp.broadcast_to(jnp.where(m1, 1.0, 0.0), (TOK, 128)).astype(BF)
+        m0 = id0 == float(e)
+        m1 = id1 == float(e)
+        f0 = jnp.where(m0, 1.0, 0.0).astype(BF)
+        f1 = jnp.where(m1, 1.0, 0.0).astype(BF)
         for n in range(HEADS):
             c = slice(n * HD, (n + 1) * HD)
             oe[e, :, c] = o_ref[:, c] * f0 + o_ref[:, half + n * HD:half + (n + 1) * HD] * f1
-        gate = jnp.where(m0, meta_ref[:, 2:3], jnp.where(m1, meta_ref[:, 3:4], 0.0))
-        gb[e] = jnp.broadcast_to(gate, (TOK, 128))
+        gb[e] = jnp.where(m0, g0, jnp.where(m1, g1, 0.0))
 
     def project(j, fresh):
         wo_copy(j).wait()
@@ -431,7 +434,7 @@
 NF = FFN // FB
 DB = 512
 ND = HID // DB
-ROW_STEPS = (128, 192, 256, 320, 384, 512)
+ROW_STEPS = (128, 160, 192, 256, 288, 320, 352, 384, 512)
 
 
 def experts_kernel(xm_ref, gain_ref, router_ref, ids_ref, wg_hbm, wu_hbm, wd_hbm, y_ref,
@@ -484,11 +487,11 @@
         spread[e] = sel.T.astype(BF)
         gc[e] = jnp.broadcast_to(jnp.sum(sel * gates[e:e + 1, :], axis=1, keepdims=True), (TOK, 128))
         xc[e] = dot(pick[...], u[...]).astype(BF)
-        count[e] = (jnp.sum(hit).astype(jnp.int32) + 63) // 64
+        count[e] = (jnp.sum(hit).astype(jnp.int32) + 31) // 32
 
     def by_blocks(blocks, run):
         for low, high in zip((0,) + ROW_STEPS[:-1], ROW_STEPS):
-            @pl.when((blocks * 64 > low) & (blocks * 64 <= high) if low else blocks * 64 <= high)
+            @pl.when((blocks * 32 > low) & (blocks * 32 <= high) if low else blocks * 32 <= high)
             def _(high=high):
                 run(high)
 
@@ -592,11 +595,11 @@
     width = HID // chunks
     return pl.pallas_call(
         sum_kernel,
-        out_shape=jax.ShapeDtypeStruct((TOK, HID), BF),
+        out_shape=pltpu.VMEM((TOK, HID), BF),
         in_specs=[hspec(), hspec()],
         out_specs=vspec(),
         scratch_shapes=[pltpu.VMEM((TOK, HID), BF), pltpu.VMEM((TOK, HID), BF), pltpu.SemaphoreType.DMA((2,))] + pair_scratch(chunks, width),
-        compiler_params=pltpu.CompilerParams(vmem_limit_bytes=61 * 1024 * 1024, collective_id=1, has_side_effects=True),
+        compiler_params=pltpu.CompilerParams(vmem_limit_bytes=57 * 1024 * 1024, collective_id=1, has_side_effects=True),
         name="expert_sum",
     )(xm, y)
 

time: 158 us -> 151 us (0.956); the launches traced: 159 us -> 150 us
  Pallas kernels: 155 us -> 148 us
  local copies, waits for them, and re-layouts: 3.16 us -> 1.32 us
    pallas_call x1, Pallas kernels: 36.1 us -> 28.3 us  [sum_call(): pl.pallas_call(sum_kernel, out_shape=pltpu.VMEM((TOK, HID), BF), in_specs...]
    pallas_call x1, Pallas kernels: 46.4 us -> 49.3 us  [experts_call(): pl.pallas_call(experts_kernel, out_shape=jax.ShapeDtypeStruct((TOK, HID),...]
    unnamed x1, local copies, waits for them, and re-layouts: 3.16 us -> 1.32 us
where the time goes in v4:
time: 151 us; the launch traced here: 150 us
  Pallas kernels  148 us (98%)
    pallas_call x1, Pallas kernels, experts_call(): pl.pallas_call(experts_kernel, out_shape=jax.ShapeDtypeStruct((TOK, HID),...  49.3 us
    pallas_call x1, Pallas kernels, project_call(): pl.pallas_call(project_kernel, out_shape=jax.ShapeDtypeStruct((TOK, HID),...  36.1 us
    pallas_call x1, Pallas kernels, attention_call(): pl.pallas_call(attention_kernel, out_shape=(cache, cache, jax.ShapeDtypeS...  33.9 us
    pallas_call x1, Pallas kernels, sum_call(): pl.pallas_call(sum_kernel, out_shape=pltpu.VMEM((TOK, HID), BF), in_specs...  28.3 us

profile of v4, /device:TPU:0, one launch (start us, length us, event | category | flops | bytes accessed | tf_op | source)
XLA Modules:
  0.0 149.5 jit_solution(3900699296277992077)
XLA Ops:
  0.6 33.9 %attention.1 = (bf16[32768,128]{1,0:T(8,128)(2,1)}, bf16[32768,128]{1,0:T(8,128)(2,1)}, bf16[512,1024]{1,0:T(8,128)(2,1)}, f32[512,128]{1,0:T(8,128)}) custom-call(bf16[512,2048]{1,0:T(8,128)(2,1)} %x_hbm.1, f32[1,2048]{1,0:T(1,128)} %bitcast.21, bf16[16384,128]{1,0:T(8,128)(2,1)} %bitcast.18, bf16[8,2048]{1,0:T(8,128)(2,1)} %bitcast.19, ...), custom_call_target="tpu_custom_call" | custom-call | tf_op jit(solution)/shard_map/attention/pallas_call | solution.py:250
  34.5 36.1 %project_sum.1.xm_ref.xm_hbm = bf16[512,2048]{1,0:T(8,128)(2,1)} custom-call(bf16[512,2048]{1,0:T(8,128)(2,1)} %x_hbm.1, bf16[512,1024]{1,0:T(8,128)(2,1)} %get-tuple-element.7.o_ref, f32[512,128]{1,0:T(8,128)} %get-tuple-element.8.meta_ref, bf16[8,512,2048]{2,1,0:T(8,128)(2,1)} %wo_hbm.1), custom_call_target="tpu_custom_call" | custom-call | tf_op jit(solution)/shard_map/project_sum/pallas_call | solution.py:414
  70.7 49.3 %experts.1.y_hbm = bf16[512,2048]{1,0:T(8,128)(2,1)} custom-call(bf16[512,2048]{1,0:T(8,128)(2,1)} %project_sum.1.xm_ref.xm_hbm, f32[1,2048]{1,0:T(1,128)} %bitcast.22, bf16[8,2048]{1,0:T(8,128)(2,1)} %bitcast.20, s32[2,512]{1,0:T(2,128)} %bitcast.24, bf16[2,2048,5632]{2,1,0:T(8,128)(2,1)} %wg_hbm.1, bf16[2,2048,5632]{2,1,0:T(8,128)(2,1)} %wu_hbm.1, ...), custom_call_target="tpu_custom_call" | custom-call | tf_op jit(solution)/shard_map/experts/pallas_call | solution.py:550
  119.9 28.3 %expert_sum.1 = bf16[512,2048]{1,0:T(8,128)(2,1)S(1)} custom-call(bf16[512,2048]{1,0:T(8,128)(2,1)} %project_sum.1.xm_ref.xm_hbm, bf16[512,2048]{1,0:T(8,128)(2,1)} %experts.1.y_hbm), custom_call_target="tpu_custom_call" | custom-call | tf_op jit(solution)/shard_map/expert_sum/pallas_call | solution.py:596
  148.2 1.3 copy.23

commit v5 on v4

--- a/solution.py
+++ b/solution.py
@@ -293,7 +293,9 @@
         barrier = pltpu.get_barrier_semaphore()
         for d in (self.sib, self.peer):
             pl.semaphore_signal(barrier, inc=1, device_id={"tp": d}, device_id_type=MESH)
-        pl.semaphore_wait(barrier, 2)
+
+    def meet(self):
+        pl.semaphore_wait(pltpu.get_barrier_semaphore(), 2)
 
     def cols(self, j):
         return pl.ds(pl.multiple_of(j * self.width, self.width), self.width)
@@ -372,8 +374,6 @@
         wo_copy(j).wait()
         slot = j % ring
         for e in range(ATT_E):
-            if fresh:
-                prepare(e)
             prod = dot(oe[e], wo[slot, e])
             for n in range(width // 128):
                 c = slice(n * 128, (n + 1) * 128)
@@ -384,6 +384,8 @@
                     acc[:, c] += term
                 else:
                     part[j, :, c] = (acc[:, c] + term).astype(BF)
+        if fresh:
+            net.meet()
         net.first(j)
 
     def chunk_step(j, _):
@@ -398,6 +400,8 @@
             net.second(j - 1)
         return 0
 
+    for e in range(ATT_E):
+        prepare(e)
     project(0, True)
     wo_copy(ring).start()
     net.second(0)
@@ -576,6 +580,7 @@
     y_copy.start()
     x_copy.start()
     net.greet()
+    net.meet()
     for j in range(chunks):
         net.first(j)
     y_copy.wait()

time: 151 us -> 149 us (0.987)
  Pallas kernels: 148 us -> 146 us
    pallas_call x1, Pallas kernels: 28.3 us -> 31.1 us  [sum_call(): pl.pallas_call(sum_kernel, out_shape=pltpu.VMEM((TOK, HID), BF), in_specs...]
    pallas_call x1, Pallas kernels: 49.3 us -> 46.4 us  [experts_call(): pl.pallas_call(experts_kernel, out_shape=jax.ShapeDtypeStruct((TOK, HID),...]
where the time goes in v5:
time: 149 us; the launch traced here: 148 us
  Pallas kernels  146 us (98%)
    pallas_call x1, Pallas kernels, experts_call(): pl.pallas_call(experts_kernel, out_shape=jax.ShapeDtypeStruct((TOK, HID),...  46.4 us
    pallas_call x1, Pallas kernels, project_call(): pl.pallas_call(project_kernel, out_shape=jax.ShapeDtypeStruct((TOK, HID),...  35 us
    pallas_call x1, Pallas kernels, attention_call(): pl.pallas_call(attention_kernel, out_shape=(cache, cache, jax.ShapeDtypeS...  33.9 us
    pallas_call x1, Pallas kernels, sum_call(): pl.pallas_call(sum_kernel, out_shape=pltpu.VMEM((TOK, HID), BF), in_specs...  31.1 us

profile of v5, /device:TPU:0, one launch (start us, length us, event | category | flops | bytes accessed | tf_op | source)
XLA Modules:
  0.0 148.4 jit_solution(17671877698965748767)
XLA Ops:
  0.6 33.9 %attention.1 = (bf16[32768,128]{1,0:T(8,128)(2,1)}, bf16[32768,128]{1,0:T(8,128)(2,1)}, bf16[512,1024]{1,0:T(8,128)(2,1)}, f32[512,128]{1,0:T(8,128)}) custom-call(bf16[512,2048]{1,0:T(8,128)(2,1)} %x_hbm.1, f32[1,2048]{1,0:T(1,128)} %bitcast.21, bf16[16384,128]{1,0:T(8,128)(2,1)} %bitcast.18, bf16[8,2048]{1,0:T(8,128)(2,1)} %bitcast.19, ...), custom_call_target="tpu_custom_call" | custom-call | tf_op jit(solution)/shard_map/attention/pallas_call | solution.py:250
  34.5 35.0 %project_sum.1.xm_ref.xm_hbm = bf16[512,2048]{1,0:T(8,128)(2,1)} custom-call(bf16[512,2048]{1,0:T(8,128)(2,1)} %x_hbm.1, bf16[512,1024]{1,0:T(8,128)(2,1)} %get-tuple-element.7.o_ref, f32[512,128]{1,0:T(8,128)} %get-tuple-element.8.meta_ref, bf16[8,512,2048]{2,1,0:T(8,128)(2,1)} %wo_hbm.1), custom_call_target="tpu_custom_call" | custom-call | tf_op jit(solution)/shard_map/project_sum/pallas_call | solution.py:418
  69.5 46.4 %experts.1.y_hbm = bf16[512,2048]{1,0:T(8,128)(2,1)} custom-call(bf16[512,2048]{1,0:T(8,128)(2,1)} %project_sum.1.xm_ref.xm_hbm, f32[1,2048]{1,0:T(1,128)} %bitcast.22, bf16[8,2048]{1,0:T(8,128)(2,1)} %bitcast.20, s32[2,512]{1,0:T(2,128)} %bitcast.24, bf16[2,2048,5632]{2,1,0:T(8,128)(2,1)} %wg_hbm.1, bf16[2,2048,5632]{2,1,0:T(8,128)(2,1)} %wu_hbm.1, ...), custom_call_target="tpu_custom_call" | custom-call | tf_op jit(solution)/shard_map/experts/pallas_call | solution.py:554
  115.9 31.1 %expert_sum.1 = bf16[512,2048]{1,0:T(8,128)(2,1)S(1)} custom-call(bf16[512,2048]{1,0:T(8,128)(2,1)} %project_sum.1.xm_ref.xm_hbm, bf16[512,2048]{1,0:T(8,128)(2,1)} %experts.1.y_hbm), custom_call_target="tpu_custom_call" | custom-call | tf_op jit(solution)/shard_map/expert_sum/pallas_call | solution.py:601
  147.1 1.3 copy.23
